TPU v7x, 256 devices: a whole 4x4x8 slice. The times are simulated.
256 devices in a mesh: phase: 8 (over y, core), row: 32 (over z, x).
Axes of the slice: x: 4, y: 4, z: 8, core: 2. Of those that a mesh axis runs over, the one named last changes fastest.
Arguments:
- linkage: float32 [2, 8, 1024, 1024], P(None, 'phase', 'row'), as said below
- pulse: float32 [32, 5, 3], replicated, may hold values from -1.2 to 1.2
- segments: int32 [8, 2], P('phase'), may hold values from 0 to 31
- ticks: int32 [8, 2], P('phase'), may hold values from 1 to 4
- detuning: float32 [5], replicated, may hold values from -0.4 to 0.4
- level_shift: float32 [5], replicated, may hold values from -1 to 1
- coupling: float32 [4], replicated, may hold values from -0.5 to 0.5
- dephase: float32 [5], replicated, may hold values from 0.01 to 0.1
Outputs:
- link_gradient: float32 [2, 8, 1024, 1024], P(None, 'phase', 'row')
Inputs may be any that keep to these rules, and one draw needn't show every extreme that they name: Every linkage state is Hermitian: for each phase, the real part is a symmetric matrix and the imaginary part an antisymmetric one.
All inputs are finite; a program needn't handle non-finite values.
Results may differ from a plain program's by a relative error of at most 0.0003.
Values sent between devices are 32-bit elements; how exact they have to be, the bound alone decides.
No kernel may reach another device: no remote copies, remote signals or barrier semaphores. Data moves between devices by JAX's collectives and lax.ppermute only.
A program may use at most 64 MiB of HBM per device.

v0:
```python
import math

import jax
import jax.numpy as jnp
from jax import lax
from jax.experimental import pallas as pl
from jax.experimental.pallas import tpu as pltpu
from jax.sharding import PartitionSpec as P

TRANSMONS = 5
LEVELS = 4
STEPS = 2


F32 = jnp.float32
BF16 = jnp.bfloat16


def iota(shape, dim):
    return lax.broadcasted_iota(jnp.int32, shape, dim)


def sincos(x):
    q = jnp.floor(x * F32(2.0 / math.pi) + F32(0.5))
    r = x - q * F32(1.5703125)
    r = r - q * F32(4.837512969970703125e-4)
    r = r - q * F32(7.549789948768648e-8)
    z = r * r
    s = r + r * z * (F32(-1 / 6) + z * (F32(1 / 120) + z * (F32(-1 / 5040) + z * F32(1 / 362880))))
    c = F32(1.0) + z * (
        F32(-0.5) + z * (F32(1 / 24) + z * (F32(-1 / 720) + z * F32(1 / 40320)))
    )
    k = q.astype(jnp.int32)
    odd = (k & 1) == 1
    sin = jnp.where(odd, c, s)
    cos = jnp.where(odd, s, c)
    sin = jnp.where((k & 2) == 2, -sin, sin)
    cos = jnp.where(((k + 1) & 2) == 2, -cos, cos)
    return sin, cos


def split(x):
    hi = x.astype(BF16)
    return hi, (x - hi.astype(F32)).astype(BF16)


def dot(a, b, transposed=False):
    dims = (((1,), (1 if transposed else 0,)), ((), ()))
    return lax.dot_general(a, b, dims, preferred_element_type=F32)


def mm(x, hi, lo, transposed=False):
    a, b = split(x)
    return dot(a, hi, transposed) + dot(a, lo, transposed) + dot(b, hi, transposed)


def left(hi, lo, x):
    a, b = split(x)
    return dot(hi, a) + dot(hi, b) + dot(lo, a)


def pmm(x, w, transposed=False):
    a, b = split(x)
    return dot(a, w, transposed) + dot(b, w, transposed)


def pleft(w, x):
    a, b = split(x)
    return dot(w, a) + dot(w, b)


def rotation(ints, pulse, step, k, width):
    base = ints[step] * 15 + 3 * k
    sc = [sincos(jnp.full((1, width), pulse[base + m], F32)) for m in range(3)]
    (s0, c0), (s1, c1), (s2, c2) = sc
    zero = jnp.zeros((1, width), F32)
    return [
        [c0, -s0 * c1, s0 * s1 * c2, -s0 * s1 * s2],
        [s0, c0 * c1, -c0 * s1 * c2, c0 * s1 * s2],
        [zero, s1, c1 * c2, -c1 * s2],
        [zero, zero, s2, c2],
    ]


def identity(width):
    one, zero = jnp.ones((1, width), F32), jnp.zeros((1, width), F32)
    return [[one if a == b else zero for b in range(4)] for a in range(4)]


def flip(o):
    return [[o[b][a] for b in range(4)] for a in range(4)]


def pick(digit, choices):
    out = choices[3]
    for v in (2, 1, 0):
        out = jnp.where(digit == v, choices[v], out)
    return out


def lane_rows(o, lane_digit):
    return [pick(lane_digit, o[x]) for x in range(4)]


def kron_blocks(mats, lane_digits):
    width = lane_digits[0].shape[1]
    t = [lane_rows(o, d) for o, d in zip(mats, lane_digits)]
    row = iota((16, width), 0)
    low = pick(row >> 2, t[2]) * pick(row & 3, t[3])
    return [low * (t[0][a] * t[1][b]) for a in range(4) for b in range(4)]


def store_kron(hi_ref, lo_ref, mats, lane_digits):
    for n, block in enumerate(kron_blocks(mats, lane_digits)):
        hi, lo = split(block)
        hi_ref[16 * n : 16 * n + 16, :] = hi
        if lo_ref is not None:
            lo_ref[16 * n : 16 * n + 16, :] = lo


def small_table(row_digits, lane_digits, mats):
    out = None
    for o, rd, ld in zip(mats, row_digits, lane_digits):
        part = pick(rd, lane_rows(o, ld))
        out = part if out is None else out * part
    return out


def fnum(x):
    return x.astype(F32)


def node_energy(fl, k, n):
    return fl[k] * (n * (n - F32(1.0)) * F32(0.5))


def drive_weight(n):
    return n * (n + F32(1.0)) * F32(0.5)


def table_a_kernel(ints, fl, pulse, w1h, w1l, w2h, w2l, wp, r1, r2, far, fai, o0):
    w = 256
    lane = iota((1, w), 1)
    natural = [(lane >> 6) & 3, (lane >> 4) & 3, (lane >> 2) & 3, lane & 3]
    moved = [
        (lane >> 3) & 3,
        (lane >> 1) & 3,
        (lane >> 6) & 3,
        ((lane >> 5) & 1) * 2 + (lane & 1),
    ]
    eye = identity(w)
    first = [rotation(ints, pulse, 0, k, w) for k in range(TRANSMONS)]
    second = {k: rotation(ints, pulse, 1, k, w) for k in (3, 4)}
    store_kron(w1h, w1l, [flip(first[k]) for k in (1, 2, 3, 4)], natural)
    store_kron(w2h, w2l, [eye, eye, flip(second[3]), flip(second[4])], moved)
    store_kron(wp, None, [eye] * 4, moved)
    for a in range(4):
        for b in range(4):
            o0[4 * a + b : 4 * a + b + 1, :] = first[0][a][b]
    rl = iota((1, 32), 1)
    rr = iota((32, 32), 0)
    one = [[e[:, :32] for e in row] for row in eye]
    f3 = [[e[:, :32] for e in row] for row in first[3]]
    f4 = [[e[:, :32] for e in row] for row in first[4]]
    g4 = [[e[:, :32] for e in row] for row in second[4]]
    nat_r = [rr >> 4, (rr >> 2) & 3, rr & 3]
    nat_l = [rl >> 4, (rl >> 2) & 3, rl & 3]
    mov_r = [(rr >> 2) & 1, rr & 3, rr >> 3]
    mov_l = [(rl >> 2) & 1, rl & 3, rl >> 3]
    tables = [
        small_table(nat_r, nat_l, [one, f3, f4]),
        small_table(nat_r, nat_l, [one, flip(f3), flip(f4)]),
    ]
    for n, t in enumerate(tables):
        hi, lo = split(t)
        r1[2 * n], r1[2 * n + 1] = hi, lo
    tables = [
        small_table(mov_r, nat_l, [one, one, g4]),
        small_table(nat_r, mov_l, [one, one, flip(g4)]),
        small_table(mov_r, nat_l, [one, one, one]),
        small_table(nat_r, mov_l, [one, one, one]),
    ]
    for n, t in enumerate(tables):
        hi, lo = split(t)
        r2[2 * n], r2[2 * n + 1] = hi, lo
    t12 = F32(0.5) * (fnum(ints[2]) + fnum(ints[3]))
    row = iota((32, 128), 0)
    col = iota((1, 128), 1)
    i3, i4 = fnum((row >> 2) & 3), fnum(row & 3)
    j2, j3, j4 = fnum((col >> 4) & 3), fnum((col >> 2) & 3), fnum(col & 3)

    def node(k, n):
        return node_energy(fl, k, n) + fl[14 + k] * drive_weight(n)

    ai = t12 * (fl[8] * (i3 * i4) + node(4, i4))
    aj = t12 * (fl[7] * (j2 * j3) + fl[8] * (j3 * j4) + node(3, j3) + node(4, j4))
    mag = jnp.exp(
        -t12 * (fl[12] * ((i3 - j3) * (i3 - j3)) + fl[13] * ((i4 - j4) * (i4 - j4)))
    )
    si, ci = sincos(ai)
    sj, cj = sincos(aj)
    far[...] = mag * (ci * cj + si * sj)
    fai[...] = mag * (ci * sj - si * cj)


def start_of(ints, gathered):
    rows = iota((8, 2), 0)
    kept = jnp.where(rows < ints[5], gathered[...], 0).astype(F32)
    return jnp.sum(jnp.sum(kept, axis=1, keepdims=True), axis=0, keepdims=True)


def drive_phase(fl, k, time):
    phi = time * fl[14 + k]
    turns = jnp.floor(phi * F32(0.5 / math.pi) + F32(0.5))
    return phi - turns * F32(6.28125) - turns * F32(2 * math.pi - 6.28125)


def energy_of(fl, digits):
    total = node_energy(fl, 0, digits[0])
    for k in range(1, TRANSMONS):
        total = total + node_energy(fl, k, digits[k])
    for k in range(TRANSMONS - 1):
        total = total + fl[5 + k] * (digits[k] * digits[k + 1])
    return total


def factor_parts(fl, span, sign, time, row_digits, col_digits):
    phis = [drive_phase(fl, k, time) for k in range(TRANSMONS)]

    def angle(digits):
        total = (F32(0.5) * span) * energy_of(fl, digits)
        drive = phis[0] * drive_weight(digits[0])
        for k in range(1, TRANSMONS):
            drive = drive + phis[k] * drive_weight(digits[k])
        return total + drive if sign > 0 else total - drive

    return sincos(angle(row_digits)), sincos(angle(col_digits))


def decay_of(fl, row_digits, col_digits):
    total = None
    for k in range(TRANSMONS):
        gap = row_digits[k] - col_digits[k]
        part = fl[9 + k] * (gap * gap)
        total = part if total is None else total + part
    return total


def first_factor(ints, fl, gathered):
    span = fnum(ints[2])
    time = start_of(ints, gathered) + F32(0.5) * span
    row = ints[4] * 32 + iota((32, 128), 0)
    col = iota((1, 1024), 1)
    rd = [fnum((row >> (8 - 2 * k)) & 3) for k in range(TRANSMONS)]
    cd = [fnum((col >> (8 - 2 * k)) & 3) for k in range(TRANSMONS)]
    (si, ci), (sj, cj) = factor_parts(fl, span, 1, time, rd, cd)
    wide = [jnp.concatenate([d] * 8, axis=1) for d in rd]
    mag = jnp.exp(F32(-0.5) * span * decay_of(fl, wide, cd))
    si, ci = jnp.concatenate([si] * 8, axis=1), jnp.concatenate([ci] * 8, axis=1)
    return mag * (ci * cj + si * sj), mag * (ci * sj - si * cj)


def to_rows(blocks):
    return jnp.concatenate(
        [
            blocks[:, c * 1024 + a * 256 : c * 1024 + a * 256 + 256]
            for a in range(4)
            for c in range(2)
        ],
        axis=0,
    )


def to_lanes(rows):
    return jnp.concatenate(
        [rows[(2 * a + c) * 32 : (2 * a + c) * 32 + 32, :] for c in range(2) for a in range(4)],
        axis=1,
    )


def mix_top(o0, rows, transposed):
    out = []
    for a in range(4):
        total = None
        for b in range(4):
            n = 4 * b + a if transposed else 4 * a + b
            part = rows[64 * b : 64 * b + 64, :] * o0[n : n + 1, :]
            total = part if total is None else total + part
        out.append(total)
    return jnp.concatenate(out, axis=0)


def chunk_of_lane(shape):
    return (iota(shape, 1) >> 5) & 3


def send(out, offset, x):
    for c in range(2):
        for half in range(2):
            tiles = [
                x[:, c * 1024 + a * 256 + half * 128 : c * 1024 + a * 256 + half * 128 + 128]
                for a in range(4)
            ]
            chunk = chunk_of_lane((32, 128))
            for q in range(4):
                moved = [
                    tiles[a] if a == q else pltpu.roll(tiles[a], ((a - q) * 32) % 128, 1)
                    for a in range(4)
                ]
                merged = pick(chunk, moved)
                for i4 in range(4):
                    out[i4 * 8 + half * 4 + q, :, offset + c * 128 : offset + c * 128 + 128] = (
                        merged[i4 * 8 : i4 * 8 + 8, :]
                    )


def receive(ref, offset):
    chunk = chunk_of_lane((32, 128))
    pieces = {}
    for c in range(2):
        for half in range(2):
            merged = [
                jnp.concatenate(
                    [
                        ref[i4 * 8 + half * 4 + q, :, offset + c * 128 : offset + c * 128 + 128]
                        for i4 in range(4)
                    ],
                    axis=0,
                )
                for q in range(4)
            ]
            for a in range(4):
                moved = [
                    merged[q] if a == q else pltpu.roll(merged[q], ((q - a) * 32) % 128, 1)
                    for q in range(4)
                ]
                pieces[c, a, half] = pick(chunk, moved)
    return jnp.concatenate(
        [pieces[c, a, half] for c in range(2) for a in range(4) for half in range(2)], axis=1
    )


def apply_pointwise_a(rows, far, fai, conj):
    fr = jnp.concatenate([far, far], axis=1)
    fi = jnp.concatenate([fai, fai], axis=1)
    if conj:
        fi = -fi
    out = []
    for a in range(4):
        re, im = rows[64 * a : 64 * a + 32, :], rows[64 * a + 32 : 64 * a + 64, :]
        out += [re * fr - im * fi, re * fi + im * fr]
    return jnp.concatenate(out, axis=0)


def forward_a_kernel(
    ints, fl, gathered, x, f, w1h, w1l, w2h, w2l, wp, r1, r2, far, fai, o0, out
):
    fr, fi = first_factor(ints, fl, gathered)
    re, im = x[0], x[1]
    both = jnp.concatenate([re * fr - im * fi, re * fi + im * fr], axis=1)
    both = left(r1[0], r1[1], both)
    rows = mix_top(o0, to_rows(both), False)
    rows = mm(rows, w1h[...], w1l[...])
    rows = apply_pointwise_a(rows, far[...], fai[...], False)
    rows = mm(rows, w2h[...], w2l[...])
    send(out, 0, left(r2[0], r2[1], to_lanes(rows)))
    rows = to_rows(jnp.concatenate([f[0], f[1]], axis=1))
    send(out, 256, pleft(r2[4], to_lanes(pmm(rows, wp[...]))))


def adjoint_a_kernel(
    ints, fl, gathered, y, m, w1h, w1l, w2h, w2l, wp, r1, r2, far, fai, o0, out
):
    rows = to_rows(left(r2[2], r2[3], receive(y, 0)))
    rows = mm(rows, w2h[...], w2l[...], True)
    rows = apply_pointwise_a(rows, far[...], fai[...], True)
    rows = mm(rows, w1h[...], w1l[...], True)
    rows = mix_top(o0, rows, True)
    both = left(r1[2], r1[3], to_lanes(rows))
    fr, fi = first_factor(ints, fl, gathered)
    re, im = both[:, :1024], both[:, 1024:]
    other = to_lanes(pmm(to_rows(pleft(r2[6], receive(m, 0))), wp[...], True))
    out[0] = re * fr + im * fi - other[:, :1024]
    out[1] = im * fr - re * fi - other[:, 1024:]


def table_b_kernel(
    ints, fl, gathered, pulse, a1h, a1l, b1h, b1l, a2h, a2l, b2h, b2l, vh, vl, fmr, fmi, ffr, ffi
):
    w = 256
    lane = iota((1, w), 1)
    natural = [(lane >> 6) & 3, (lane >> 4) & 3, (lane >> 2) & 3, lane & 3]
    eye = identity(w)
    first = [rotation(ints, pulse, 0, k, w) for k in range(3)]
    second = [rotation(ints, pulse, 1, k, w) for k in range(4)]
    store_kron(a1h, a1l, [*first, eye], natural)
    store_kron(b1h, b1l, [*(flip(o) for o in first), eye], natural)
    store_kron(a2h, a2l, second, natural)
    store_kron(b2h, b2l, [flip(o) for o in second], natural)
    row = iota((16, w), 0)
    cl, l0, l1, l2, ll = (lane >> 7), (lane >> 5) & 3, (lane >> 3) & 3, (lane >> 1) & 3, lane & 1
    t0 = lane_rows(flip(second[0]), l0)
    t1 = lane_rows(flip(second[1]), l1)
    t2 = lane_rows(flip(second[2]), l2)
    low = pick((row >> 1) & 3, t2) * jnp.where((row & 1) == ll, F32(1.0), F32(0.0))
    high_bit = row >> 3
    for n in range(16):
        c, d0, top = n >> 3, (n >> 1) & 3, n & 1
        mid = jnp.where(high_bit == 0, t1[2 * top], t1[2 * top + 1])
        block = low * mid * (t0[d0] * jnp.where(cl == c, F32(1.0), F32(0.0)))
        hi, lo = split(block)
        vh[16 * n : 16 * n + 16, :] = hi
        vl[16 * n : 16 * n + 16, :] = lo
    row = iota((256, 128), 0)
    col = iota((1, 128), 1)
    rd = [fnum((row >> (6 - 2 * k)) & 3) for k in range(4)]
    cd = [fnum((col >> 5) & 3), fnum((col >> 3) & 3), fnum((col >> 1) & 3)]
    t12 = F32(0.5) * (fnum(ints[2]) + fnum(ints[3]))

    def node(k, n):
        return node_energy(fl, k, n) + fl[14 + k] * drive_weight(n)

    ai = fl[5] * (rd[0] * rd[1]) + fl[6] * (rd[1] * rd[2]) + fl[7] * (rd[2] * rd[3])
    for k in range(4):
        ai = ai + node(k, rd[k])
    aj = fl[5] * (cd[0] * cd[1]) + fl[6] * (cd[1] * cd[2])
    for k in range(3):
        aj = aj + node(k, cd[k])
    gap = None
    for k in range(3):
        part = fl[9 + k] * ((rd[k] - cd[k]) * (rd[k] - cd[k]))
        gap = part if gap is None else gap + part
    mag = jnp.exp(-t12 * gap)
    si, ci = sincos(t12 * ai)
    sj, cj = sincos(t12 * aj)
    fmr[...] = mag * (ci * cj + si * sj)
    fmi[...] = mag * (ci * sj - si * cj)
    rank = ints[4]
    i4 = fnum(jnp.full((256, 128), rank >> 3, jnp.int32))
    j3 = fnum(jnp.full((1, 128), (rank >> 1) & 3, jnp.int32))
    j4 = fnum((rank & 1) * 2 + (col & 1))
    rows = [*rd, i4]
    cols = [*cd, j3, j4]
    span = fnum(ints[3])
    time = start_of(ints, gathered) + (fnum(ints[2]) + F32(0.5) * span)
    (si, ci), (sj, cj) = factor_parts(fl, span, -1, time, rows, cols)
    mag = jnp.exp(F32(-0.5) * span * decay_of(fl, rows, cols))
    ffr[...] = mag * (ci * cj + si * sj)
    ffi[...] = mag * (ci * sj - si * cj)


def cmul(x, fr, fi, conj=False):
    re, im = x[:, :128], x[:, 128:]
    if conj:
        return jnp.concatenate([re * fr + im * fi, im * fr - re * fi], axis=1)
    return jnp.concatenate([re * fr - im * fi, re * fi + im * fr], axis=1)


def both_b_kernel(x, a1h, a1l, b1h, b1l, a2h, a2l, b2h, b2l, vh, vl, fmr, fmi, ffr, ffi, out):
    z = left(a1h[...], a1l[...], x[:, :256])
    z = cmul(z, fmr[...], fmi[...])
    z = left(a2h[...], a2l[...], z)
    z = mm(z, vh[...], vl[...])
    z = cmul(z, ffr[...], ffi[...]) - x[:, 256:]
    out[:, 256:] = z
    z = cmul(z, ffr[...], ffi[...], True)
    z = left(b2h[...], b2l[...], z)
    z = mm(z, vh[...], vl[...], True)
    z = cmul(z, fmr[...], fmi[...], True)
    out[:, :256] = left(b1h[...], b1l[...], z)


SMEM = pl.BlockSpec(memory_space=pltpu.SMEM)
VMEM = pl.BlockSpec(memory_space=pltpu.VMEM)


def call(kernel, args, scalars, outs, flops, name):
    specs = [SMEM if n in scalars else VMEM for n in range(len(args))]
    return pl.pallas_call(
        kernel,
        in_specs=specs,
        out_specs=jax.tree.map(lambda _: VMEM, outs),
        out_shape=outs,
        name=name,
        cost_estimate=pl.CostEstimate(flops=flops, transcendentals=0, bytes_accessed=1 << 20),
    )(*args)


def sds(*shape, dtype=F32):
    return jax.ShapeDtypeStruct(shape, dtype)


def local(linkage, pulse, segments, ticks, detuning, level_shift, coupling, dephase):
    current = linkage[:, 0]
    phases = lax.axis_size("phase")
    ints = jnp.concatenate(
        [
            segments[0],
            ticks[0],
            jnp.stack([lax.axis_index("row"), lax.axis_index("phase")]).astype(jnp.int32),
        ]
    )
    floats = jnp.concatenate([level_shift, coupling, dephase, detuning])
    flat_pulse = pulse.reshape(-1)
    gathered = lax.all_to_all(
        jnp.broadcast_to(ticks, (phases, STEPS)), "phase", split_axis=0, concat_axis=0, tiled=True
    )
    following = lax.ppermute(
        current, "phase", [((i + 1) % phases, i) for i in range(phases)]
    )
    square = sds(256, 256, dtype=BF16)
    tables_a = call(
        table_a_kernel,
        (ints, floats, flat_pulse),
        (0, 1, 2),
        (
            *([square] * 5),
            sds(4, 32, 32, dtype=BF16),
            sds(8, 32, 32, dtype=BF16),
            sds(32, 128),
            sds(32, 128),
            sds(16, 256),
        ),
        1 << 28,
        "table_a",
    )
    sent = call(
        forward_a_kernel,
        (ints, floats, gathered, current, following, *tables_a),
        (0, 1),
        sds(32, 8, 512),
        1 << 28,
        "forward_a",
    )
    turned = lax.all_to_all(sent, "row", split_axis=0, concat_axis=0, tiled=True)
    tables_b = call(
        table_b_kernel,
        (ints, floats, gathered, flat_pulse),
        (0, 1, 3),
        (*([square] * 10), *([sds(256, 128)] * 4)),
        1 << 30,
        "table_b",
    )
    back = call(
        both_b_kernel,
        (turned.reshape(256, 512), *tables_b),
        (),
        sds(256, 512),
        1 << 28,
        "both_b",
    )
    returned = lax.all_to_all(
        back.reshape(32, 8, 512), "row", split_axis=0, concat_axis=0, tiled=True
    )
    earlier = lax.ppermute(
        returned[:, :, 256:], "phase", [(i, (i + 1) % phases) for i in range(phases)]
    )
    result = call(
        adjoint_a_kernel,
        (ints, floats, gathered, returned, earlier, *tables_a),
        (0, 1),
        sds(2, 32, 1024),
        1 << 28,
        "adjoint_a",
    )
    return result[:, None]


def solution(mesh):
    return jax.shard_map(
        local,
        mesh=mesh,
        in_specs=(
            P(None, "phase", "row", None),
            P(),
            P("phase", None),
            P("phase", None),
            P(),
            P(),
            P(),
            P(),
        ),
        out_specs=P(None, "phase", "row", None),
        check_vma=False,
    )
```

profile of v0, /device:TPU:32, one launch (start us, length us, event | category | flops | bytes accessed | tf_op | source)
XLA Modules:
  0.0 83.4 jit_solution(5366910189361864977)
XLA Ops:
  0.0 0.0 copy-start.6
  0.0 2.5 %collective-permute-start = (f32[2,32,1024]{2,1,0:T(8,128)}, f32[2,32,1024]{2,1,0:T(8,128)S(1)}, u32[]{:S(2)}, u32[]{:S(2)}) collective-permute-start(f32[2,32,1024]{2,1,0:T(8,128)} %bitcast.13), channel_id=1, source_target_pairs={{32,0},{64,32},{96,64},{128,96},{160,128},{192,160},{224,192},{0,2... | collective-permute-start | bytes 786440 | tf_op jit(solution)/shard_map/ppermute | solution.py:508
  2.5 0.0 copy-done.6
  2.5 0.6 broadcast_in_dim.8
  3.1 0.0 copy-start.5
  3.1 3.4 %all-to-all-start = ((s32[8,1,2]{2,1,0:T(1,128)}), s32[8,1,2]{2,1,0:T(1,128)S(1)}, u32[]{:S(2)}, u32[]{:S(2)}) async-start(s32[8,1,2]{2,1,0:T(1,128)} %broadcast_in_dim.8), calls=%async_computation | async-start | bytes 8192 | tf_op jit(solution)/shard_map/all_to_all | solution.py:505
  6.5 0.0 copy-done.5
  6.5 0.1 copy.19
  6.7 0.8 reshape.15.pulse
  7.4 0.0 copy-start.7
  7.4 0.7 copy-done.7
  8.1 0.0 copy-start.8
  8.1 0.0 copy-start.9
  8.1 0.0 copy-start.10
  8.1 0.0 copy-start.11
  8.1 0.7 pad_add_fusion.ints
  8.8 0.0 copy-done.8
  8.8 0.0 copy-done.9
  8.8 0.0 copy-done.10
  8.8 0.0 copy-done.11
  8.8 0.7 pad_maximum_fusion.fl
  9.5 1.9 %table_a.1 = (bf16[256,256]{1,0:T(8,128)(2,1)}, bf16[256,256]{1,0:T(8,128)(2,1)}, bf16[256,256]{1,0:T(8,128)(2,1)}, bf16[256,256]{1,0:T(8,128)(2,1)}, bf16[256,2...) custom-call(s32[6]{0:T(128)} %pad_add_fusion.ints, ...), custom_call_target="tpu_custom_call" | custom-call | flops 268435456 | bytes 1048576 | tf_op jit(solution)/shard_map/table_a/pallas_call | solution.py:479
  11.4 0.3 all-to-all-done
  11.6 0.0 copy-start.4
  11.6 0.0 collective-permute-done.f
  11.6 0.0 copy-start.2
  11.7 0.6 copy-done.4
  12.2 0.1 copy-done.2
  12.4 4.1 %forward_a.1 = f32[32,8,512]{2,1,0:T(8,128)} custom-call(s32[6]{0:T(128)} %pad_add_fusion.ints, f32[19]{0:T(128)} %pad_maximum_fusion.fl, s32[8,2]{1,0:T(8,128)} %bitcast.15, f32[2,32,1024]{2,1,0:T(8,128)} %bitcast.14, f32[2,32,1024]{2,1,0:T(8,128)} %copy-done.2, bf16[256,256]{1,0:T(8,128)(2,1)} %get-tuple-element.29.w1h, ...), custom_call_target="tpu_custom_call" | custom-call | flops 268435456 | bytes 1048576 | tf_op jit(solution)/shard_map/forward_a/pallas_call | solution.py:479
  16.4 11.2 %all-to-all-start.1 = ((f32[32,8,512]{2,1,0:T(8,128)}), f32[32,8,512]{2,1,0:T(8,128)S(1)}, u32[]{:S(2)}, u32[]{:S(2)}) async-start(f32[32,8,512]{2,1,0:T(8,128)} %forward_a.1), calls=%async_computation.1 | async-start | bytes 1048576 | tf_op jit(solution)/shard_map/all_to_all | solution.py:535
  27.6 3.2 %table_b.1 = (bf16[256,256]{1,0:T(8,128)(2,1)}, bf16[256,256]{1,0:T(8,128)(2,1)}, bf16[256,256]{1,0:T(8,128)(2,1)}, bf16[256,256]{1,0:T(8,128)(2,1)}, bf16[256,2...) custom-call(s32[6]{0:T(128)} %pad_add_fusion.ints, ...), custom_call_target="tpu_custom_call" | custom-call | flops 1073741824 | bytes 1048576 | tf_op jit(solution)/shard_map/table_b/pallas_call | solution.py:479
  30.8 14.3 %all-to-all-done.1 = f32[32,8,512]{2,1,0:T(8,128)S(1)} async-done(((f32[32,8,512]{2,1,0:T(8,128)}), f32[32,8,512]{2,1,0:T(8,128)S(1)}, u32[]{:S(2)}, u32[]{:S(2)}) %all-to-all-start.1) | async-done | bytes 524320 | tf_op jit(solution)/shard_map/all_to_all | solution.py:535
  45.1 0.0 copy-start.1
  45.1 0.8 copy-done.1
  45.9 4.3 %both_b.1 = f32[256,512]{1,0:T(8,128)} custom-call(f32[256,512]{1,0:T(8,128)} %bitcast.11, bf16[256,256]{1,0:T(8,128)(2,1)} %get-tuple-element.39.a1h, bf16[256,256]{1,0:T(8,128)(2,1)} %get-tuple-element.40.a1l, bf16[256,256]{1,0:T(8,128)(2,1)} %get-tuple-element.41.b1h, bf16[256,256]{1,0:T(8,128)(2,1)} %get-tuple-element.42.b1l, ...), custom_call_target="tpu_custom_call" | custom-call | flops 268435456 | bytes 1048576 | tf_op jit(solution)/shard_map/both_b/pallas_call | solution.py:479
  50.3 21.6 %all_to_all.18.y = f32[32,8,512]{2,1,0:T(8,128)S(1)} all-to-all(f32[32,8,512]{2,1,0:T(8,128)} %bitcast.12), channel_id=1, replica_groups=mesh['phase'=8,'row'=32] {'row'}, dimensions={0} | all-to-all | bytes 1048576 | tf_op jit(solution)/shard_map/all_to_all | solution.py:552
  71.9 0.0 copy-start
  71.9 0.0 collective-permute-start.1
  71.9 7.0 %collective-permute-done.1.m = f32[32,8,256]{2,1,0:T(8,128)S(1)} collective-permute-done((f32[32,8,256]{2,1,0:T(8,128)S(1)}, f32[32,8,256]{2,1,0:T(8,128)S(1)}, u32[]{:S(2)}, u32[]{:S(2)}) %collective-permute-start.1) | collective-permute-done | bytes 262176 | tf_op jit(solution)/shard_map/ppermute | solution.py:555
  78.9 0.0 copy-done
  78.9 0.0 copy-start.3
  78.9 0.7 copy-done.3
  79.6 3.8 %adjoint_a.1 = f32[2,32,1024]{2,1,0:T(8,128)} custom-call(s32[6]{0:T(128)} %pad_add_fusion.ints, f32[19]{0:T(128)} %pad_maximum_fusion.fl, s32[8,2]{1,0:T(8,128)} %bitcast.17, f32[32,8,512]{2,1,0:T(8,128)} %copy-done, f32[32,8,256]{2,1,0:T(8,128)} %copy-done.3, bf16[256,256]{1,0:T(8,128)(2,1)} %get-tuple-element.29.w1h, ...), custom_call_target="tpu_custom_call" | custom-call | flops 268435456 | bytes 1048576 | tf_op jit(solution)/shard_map/adjoint_a/pallas_call | solution.py:479
  (1 shorter events, 0.0 us)
Async XLA Ops:
  0.0 2.5 %copy-start.6 = (s32[1,2]{1,0:T(1,128)S(1)}, s32[1,2]{1,0:T(1,128)}, u32[]{:S(2)}) copy-start(s32[1,2]{1,0:T(1,128)} %param.11) | copy-start | bytes 28
  0.0 11.6 %collective-permute-start = (f32[2,32,1024]{2,1,0:T(8,128)}, f32[2,32,1024]{2,1,0:T(8,128)S(1)}, u32[]{:S(2)}, u32[]{:S(2)}) collective-permute-start(f32[2,32,1024]{2,1,0:T(8,128)} %bitcast.13), channel_id=1, source_target_pairs={{32,0},{64,32},{96,64},{128,96},{160,128},{192,160},{224,192},{0,2... | collective-permute-start | bytes 786440 | tf_op jit(solution)/shard_map/ppermute | solution.py:508
  3.1 3.5 %copy-start.5 = (f32[32,5,3]{0,2,1:T(4,128)S(1)}, f32[32,5,3]{0,2,1:T(4,128)}, u32[]{:S(2)}) copy-start(f32[32,5,3]{0,2,1:T(4,128)} %param.9) | copy-start | bytes 5764
  3.1 8.6 %all-to-all-start = ((s32[8,1,2]{2,1,0:T(1,128)}), s32[8,1,2]{2,1,0:T(1,128)S(1)}, u32[]{:S(2)}, u32[]{:S(2)}) async-start(s32[8,1,2]{2,1,0:T(1,128)} %broadcast_in_dim.8), calls=%async_computation | async-start | bytes 8192 | tf_op jit(solution)/shard_map/all_to_all | solution.py:505
  7.4 0.7 copy-start.7
  8.1 0.7 copy-start.8
  8.1 0.7 copy-start.9
  8.1 0.7 copy-start.10
  8.1 0.7 copy-start.11
  11.6 0.6 copy-start.4
  11.6 0.7 copy-start.2
  16.4 28.7 %all-to-all-start.1 = ((f32[32,8,512]{2,1,0:T(8,128)}), f32[32,8,512]{2,1,0:T(8,128)S(1)}, u32[]{:S(2)}, u32[]{:S(2)}) async-start(f32[32,8,512]{2,1,0:T(8,128)} %forward_a.1), calls=%async_computation.1 | async-start | bytes 1048576 | tf_op jit(solution)/shard_map/all_to_all | solution.py:535
  45.1 0.8 copy-start.1
  71.9 7.0 %copy-start = (f32[32,8,512]{2,1,0:T(8,128)}, f32[32,8,512]{2,1,0:T(8,128)S(1)}, u32[]{:S(2)}) copy-start(f32[32,8,512]{2,1,0:T(8,128)S(1)} %all_to_all.18.y) | copy-start | bytes 1572868
  71.9 7.0 %collective-permute-start.1 = (f32[32,8,256]{2,1,0:T(8,128)S(1)}, f32[32,8,256]{2,1,0:T(8,128)S(1)}, u32[]{:S(2)}, u32[]{:S(2)}) collective-permute-start(f32[32,8,256]{2,1,0:T(8,128)S(1)} %slice.4), channel_id=1, source_target_pairs={{0,32},{32,64},{64,96},{96,128},{128,160},{160,192},{192,224},{224... | collective-permute-start | bytes 786440 | tf_op jit(solution)/shard_map/ppermute | solution.py:555
  78.9 0.7 copy-start.3
where the time goes:
time: 83.9 us; the launch traced here: 83.4 us
  waiting for transfers between devices  21.6 us (26%)
  blocking collectives  21.6 us (26%)
  Pallas kernels  17.3 us (21%)
  starting transfers between devices  17.1 us (20%)
  local copies, waits for them, and re-layouts  4.43 us (5%)
  other arithmetic  1.31 us (2%)
    all_to_all x1, blocking collectives, local(): lax.all_to_all(back.reshape(32, 8, 512), 'row', split_axis=0, concat_axis...  21.6 us
    pallas_call x5, Pallas kernels, call(): pl.pallas_call(kernel, in_specs=specs, out_specs=jax.tree.map(lambda _: V...  17.3 us
    all_to_all x1, waiting for transfers between devices, local(): lax.all_to_all(sent, 'row', split_axis=0, concat_axis=0, tiled=True)  14.3 us
    all_to_all x1, starting transfers between devices, local(): lax.all_to_all(sent, 'row', split_axis=0, concat_axis=0, tiled=True)  11.2 us
    ppermute x1, waiting for transfers between devices, local(): lax.ppermute(returned[:, :, 256:], 'phase', [(i, (i + 1) % phases) for i...  6.99 us
    all_to_all x1, starting transfers between devices, local(): lax.all_to_all(jnp.broadcast_to(ticks, (phases, STEPS)), 'phase', split_a...  3.44 us
    unnamed x25, local copies, waits for them, and re-layouts  3.04 us
    ppermute x1, starting transfers between devices, local(): lax.ppermute(current, 'phase', [((i + 1) % phases, i) for i in range(phas...  2.45 us
  transfers between devices with their start and end apart: 4, of which 3 were waited for; matrix products, arithmetic and copies ran while one was open for 3% of the time, Pallas kernels for 6%

commit v1 on v0

--- a/solution.py
+++ b/solution.py
@@ -482,6 +482,7 @@
         out_specs=jax.tree.map(lambda _: VMEM, outs),
         out_shape=outs,
         name=name,
+        compiler_params=pltpu.CompilerParams(vmem_limit_bytes=16 << 20),
         cost_estimate=pl.CostEstimate(flops=flops, transcendentals=0, bytes_accessed=1 << 20),
     )(*args)
 

time: 83.9 us -> 77 us (0.918)
  Pallas kernels: 17.3 us -> 11.4 us
  waiting for transfers between devices: 21.6 us -> 24.3 us
  local copies, waits for them, and re-layouts: 4.43 us -> 2.23 us
  other arithmetic: 1.31 us -> 0.16 us
    pallas_call x5, Pallas kernels: 17.3 us -> 11.4 us  [call(): pl.pallas_call(kernel, in_specs=specs, out_specs=jax.tree.map(lambda _: V...]
    all_to_all x1, waiting for transfers between devices: 0.27 us -> 2.32 us  [local(): lax.all_to_all(jnp.broadcast_to(ticks, (phases, STEPS)), 'phase', split_a...]
    unnamed x25 -> x17, local copies, waits for them, and re-layouts: 3.04 us -> 1.41 us
  transfers between devices with their start and end apart: 4 -> 4, of which waited for: 3 -> 3; matrix products, arithmetic and copies ran while one was open for 3% -> 1% of each run, Pallas kernels for 6% -> 4%
where the time goes in v1:
time: 77 us; the launch traced here: 76.6 us
  waiting for transfers between devices  24.3 us (32%)
  blocking collectives  21.4 us (28%)
  starting transfers between devices  17.1 us (22%)
  Pallas kernels  11.4 us (15%)
  local copies, waits for them, and re-layouts  2.23 us (3%)
    all_to_all x1, blocking collectives, local(): lax.all_to_all(back.reshape(32, 8, 512), 'row', split_axis=0, concat_axis...  21.4 us
    all_to_all x1, waiting for transfers between devices, local(): lax.all_to_all(sent, 'row', split_axis=0, concat_axis=0, tiled=True)  15 us
    pallas_call x5, Pallas kernels, call(): pl.pallas_call(kernel, in_specs=specs, out_specs=jax.tree.map(lambda _: V...  11.4 us
    all_to_all x1, starting transfers between devices, local(): lax.all_to_all(sent, 'row', split_axis=0, concat_axis=0, tiled=True)  11.2 us
    ppermute x1, waiting for transfers between devices, local(): lax.ppermute(returned[:, :, 256:], 'phase', [(i, (i + 1) % phases) for i...  6.99 us
    all_to_all x1, starting transfers between devices, local(): lax.all_to_all(jnp.broadcast_to(ticks, (phases, STEPS)), 'phase', split_a...  3.44 us
    ppermute x1, starting transfers between devices, local(): lax.ppermute(current, 'phase', [((i + 1) % phases, i) for i in range(phas...  2.45 us
    all_to_all x1, waiting for transfers between devices, local(): lax.all_to_all(jnp.broadcast_to(ticks, (phases, STEPS)), 'phase', split_a...  2.32 us
  transfers between devices with their start and end apart: 4, of which 3 were waited for; matrix products, arithmetic and copies ran while one was open for 1% of the time, Pallas kernels for 4%

profile of v1, /device:TPU:32, one launch (start us, length us, event | category | flops | bytes accessed | tf_op | source)
XLA Modules:
  0.0 76.6 jit_solution(10035030904543611726)
XLA Ops:
  0.0 0.0 copy-start.2
  0.0 2.5 %collective-permute-start = (f32[2,32,1024]{2,1,0:T(8,128)}, f32[2,32,1024]{2,1,0:T(8,128)S(1)}, u32[]{:S(2)}, u32[]{:S(2)}) collective-permute-start(f32[2,32,1024]{2,1,0:T(8,128)} %bitcast.13), channel_id=1, source_target_pairs={{32,0},{64,32},{96,64},{128,96},{160,128},{192,160},{224,192},{0,2... | collective-permute-start | bytes 786440 | tf_op jit(solution)/shard_map/ppermute | solution.py:509
  2.5 0.0 copy-done.2
  2.5 0.6 broadcast_in_dim.8
  3.1 0.0 copy-start.1
  3.1 3.4 %all-to-all-start = ((s32[8,1,2]{2,1,0:T(1,128)}), s32[8,1,2]{2,1,0:T(1,128)S(1)}, u32[]{:S(2)}, u32[]{:S(2)}) async-start(s32[8,1,2]{2,1,0:T(1,128)} %broadcast_in_dim.8), calls=%async_computation | async-start | bytes 8192 | tf_op jit(solution)/shard_map/all_to_all | solution.py:506
  6.5 0.0 copy-done.1
  6.5 0.1 copy.19
  6.7 0.2 reshape.15.pulse
  6.9 0.0 copy-start.3
  6.9 0.6 copy-done.3
  7.5 0.0 copy-start.4
  7.5 0.0 copy-start.5
  7.5 0.0 copy-start.6
  7.5 0.0 copy-start.7
  7.5 0.1 pad_add_fusion.ints
  7.6 0.6 copy-done.4
  8.2 0.0 copy-done.5
  8.2 0.0 copy-done.6
  8.2 0.0 copy-done.7
  8.2 0.1 pad_maximum_fusion.fl
  8.3 0.0 copy-start
  8.3 1.0 %table_a.1 = (bf16[256,256]{1,0:T(8,128)(2,1)S(1)}, bf16[256,256]{1,0:T(8,128)(2,1)S(1)}, bf16[256,256]{1,0:T(8,128)(2,1)S(1)}, bf16[256,256]{1,0:T(8,128)(2,1)S...) custom-call(s32[6]{0:T(128)S(1)} %pad_add_fusion.ints, ...), custom_call_target="tpu_custom_call" | custom-call | flops 268435456 | bytes 1048576 | tf_op jit(solution)/shard_map/table_a/pallas_call | solution.py:479
  9.3 2.3 %all-to-all-done = s32[8,1,2]{2,1,0:T(1,128)S(1)} async-done(((s32[8,1,2]{2,1,0:T(1,128)}), s32[8,1,2]{2,1,0:T(1,128)S(1)}, u32[]{:S(2)}, u32[]{:S(2)}) %all-to-all-start) | async-done | bytes 96 | tf_op jit(solution)/shard_map/all_to_all | solution.py:506
  11.6 0.0 collective-permute-done.f
  11.6 0.0 copy-done
  11.6 3.3 %forward_a.1 = f32[32,8,512]{2,1,0:T(8,128)} custom-call(s32[6]{0:T(128)S(1)} %pad_add_fusion.ints, f32[19]{0:T(128)S(1)} %pad_maximum_fusion.fl, s32[8,2]{1,0:T(8,128)S(1)} %bitcast.15, f32[2,32,1024]{2,1,0:T(8,128)S(1)} %bitcast.14, f32[2,32,1024]{2,1,0:T(8,128)S(1)} %collective-permute-done.f, bf16[256,256]{1,0:T(8,128)(2,1)S(1)} %get-tuple-element.29.w1h, ...), custom_call_target="tpu_custom_call" | custom-call | flops 268435456 | bytes 1048576 | tf_op jit(solution)/shard_map/forward_a/pallas_call | solution.py:479
  15.0 11.2 %all-to-all-start.1 = ((f32[32,8,512]{2,1,0:T(8,128)}), f32[32,8,512]{2,1,0:T(8,128)S(1)}, u32[]{:S(2)}, u32[]{:S(2)}) async-start(f32[32,8,512]{2,1,0:T(8,128)} %forward_a.1), calls=%async_computation.1 | async-start | bytes 1048576 | tf_op jit(solution)/shard_map/all_to_all | solution.py:536
  26.2 2.2 %table_b.1 = (bf16[256,256]{1,0:T(8,128)(2,1)S(1)}, bf16[256,256]{1,0:T(8,128)(2,1)S(1)}, bf16[256,256]{1,0:T(8,128)(2,1)S(1)}, bf16[256,256]{1,0:T(8,128)(2,1)S...) custom-call(s32[6]{0:T(128)S(1)} %pad_add_fusion.ints, ...), custom_call_target="tpu_custom_call" | custom-call | flops 1073741824 | bytes 1048576 | tf_op jit(solution)/shard_map/table_b/pallas_call | solution.py:479
  28.4 15.0 %all-to-all-done.1 = f32[32,8,512]{2,1,0:T(8,128)S(1)} async-done(((f32[32,8,512]{2,1,0:T(8,128)}), f32[32,8,512]{2,1,0:T(8,128)S(1)}, u32[]{:S(2)}, u32[]{:S(2)}) %all-to-all-start.1) | async-done | bytes 524320 | tf_op jit(solution)/shard_map/all_to_all | solution.py:536
  43.3 1.8 %both_b.1 = f32[256,512]{1,0:T(8,128)S(1)} custom-call(f32[256,512]{1,0:T(8,128)S(1)} %bitcast.11, bf16[256,256]{1,0:T(8,128)(2,1)S(1)} %get-tuple-element.39.a1h, bf16[256,256]{1,0:T(8,128)(2,1)S(1)} %get-tuple-element.40.a1l, bf16[256,256]{1,0:T(8,128)(2,1)S(1)} %get-tuple-element.41.b1h, bf16[256,256]{1,0:T(8,128)(2,1)S(1)} %get-tuple-element.42.b1l, ...), custom_call_target="tpu_custom_call" | custom-call | flops 268435456 | bytes 1048576 | tf_op jit(solution)/shard_map/both_b/pallas_call | solution.py:479
  45.2 21.4 %all_to_all.18.y = f32[32,8,512]{2,1,0:T(8,128)S(1)} all-to-all(f32[32,8,512]{2,1,0:T(8,128)S(1)} %bitcast.12), channel_id=1, replica_groups=mesh['phase'=8,'row'=32] {'row'}, dimensions={0} | all-to-all | bytes 1048576 | tf_op jit(solution)/shard_map/all_to_all | solution.py:553
  66.6 0.0 collective-permute-start.1
  66.7 7.0 %collective-permute-done.1.m = f32[32,8,256]{2,1,0:T(8,128)S(1)} collective-permute-done((f32[32,8,256]{2,1,0:T(8,128)S(1)}, f32[32,8,256]{2,1,0:T(8,128)S(1)}, u32[]{:S(2)}, u32[]{:S(2)}) %collective-permute-start.1) | collective-permute-done | bytes 262176 | tf_op jit(solution)/shard_map/ppermute | solution.py:556
  73.7 3.0 %adjoint_a.1 = f32[2,32,1024]{2,1,0:T(8,128)} custom-call(s32[6]{0:T(128)S(1)} %pad_add_fusion.ints, f32[19]{0:T(128)S(1)} %pad_maximum_fusion.fl, s32[8,2]{1,0:T(8,128)S(1)} %bitcast.17, f32[32,8,512]{2,1,0:T(8,128)S(1)} %all_to_all.18.y, f32[32,8,256]{2,1,0:T(8,128)S(1)} %collective-permute-done.1.m, bf16[256,256]{1,0:T(8,128)(2,1)S(1)} %get-tuple-element.29.w1h, ...), custom_call_target="tpu_custom_call" | custom-call | flops 268435456 | bytes 1048576 | tf_op jit(solution)/shard_map/adjoint_a/pallas_call | solution.py:479
  (1 shorter events, 0.0 us)
Async XLA Ops:
  0.0 2.5 %copy-start.2 = (s32[1,2]{1,0:T(1,128)S(1)}, s32[1,2]{1,0:T(1,128)}, u32[]{:S(2)}) copy-start(s32[1,2]{1,0:T(1,128)} %param.11) | copy-start | bytes 28
  0.0 11.6 %collective-permute-start = (f32[2,32,1024]{2,1,0:T(8,128)}, f32[2,32,1024]{2,1,0:T(8,128)S(1)}, u32[]{:S(2)}, u32[]{:S(2)}) collective-permute-start(f32[2,32,1024]{2,1,0:T(8,128)} %bitcast.13), channel_id=1, source_target_pairs={{32,0},{64,32},{96,64},{128,96},{160,128},{192,160},{224,192},{0,2... | collective-permute-start | bytes 786440 | tf_op jit(solution)/shard_map/ppermute | solution.py:509
  3.1 3.5 %copy-start.1 = (f32[32,5,3]{0,2,1:T(4,128)S(1)}, f32[32,5,3]{0,2,1:T(4,128)}, u32[]{:S(2)}) copy-start(f32[32,5,3]{0,2,1:T(4,128)} %param.9) | copy-start | bytes 5764
  3.1 8.6 %all-to-all-start = ((s32[8,1,2]{2,1,0:T(1,128)}), s32[8,1,2]{2,1,0:T(1,128)S(1)}, u32[]{:S(2)}, u32[]{:S(2)}) async-start(s32[8,1,2]{2,1,0:T(1,128)} %broadcast_in_dim.8), calls=%async_computation | async-start | bytes 8192 | tf_op jit(solution)/shard_map/all_to_all | solution.py:506
  6.9 0.7 copy-start.3
  7.5 0.7 copy-start.4
  7.5 0.7 copy-start.5
  7.5 0.7 copy-start.6
  7.5 0.7 copy-start.7
  8.3 3.3 %copy-start = (f32[2,1,32,1024]{3,2,1,0:T(8,128)S(1)}, f32[2,1,32,1024]{3,2,1,0:T(8,128)}, u32[]{:S(2)}) copy-start(f32[2,1,32,1024]{3,2,1,0:T(8,128)} %param.8) | copy-start | bytes 786436
  15.0 28.4 %all-to-all-start.1 = ((f32[32,8,512]{2,1,0:T(8,128)}), f32[32,8,512]{2,1,0:T(8,128)S(1)}, u32[]{:S(2)}, u32[]{:S(2)}) async-start(f32[32,8,512]{2,1,0:T(8,128)} %forward_a.1), calls=%async_computation.1 | async-start | bytes 1048576 | tf_op jit(solution)/shard_map/all_to_all | solution.py:536
  66.6 7.0 %collective-permute-start.1 = (f32[32,8,256]{2,1,0:T(8,128)S(1)}, f32[32,8,256]{2,1,0:T(8,128)S(1)}, u32[]{:S(2)}, u32[]{:S(2)}) collective-permute-start(f32[32,8,256]{2,1,0:T(8,128)S(1)} %slice.4), channel_id=1, source_target_pairs={{0,32},{32,64},{64,96},{96,128},{128,160},{160,192},{192,224},{224... | collective-permute-start | bytes 786440 | tf_op jit(solution)/shard_map/ppermute | solution.py:556

commit v2 on v1

--- a/solution.py
+++ b/solution.py
@@ -70,8 +70,7 @@
 
 
 def rotation(ints, pulse, step, k, width):
-    base = ints[step] * 15 + 3 * k
-    sc = [sincos(jnp.full((1, width), pulse[base + m], F32)) for m in range(3)]
+    sc = [sincos(jnp.full((1, width), pulse[k, m, ints[step]], F32)) for m in range(3)]
     (s0, c0), (s1, c1), (s2, c2) = sc
     zero = jnp.zeros((1, width), F32)
     return [
@@ -114,8 +113,7 @@
     for n, block in enumerate(kron_blocks(mats, lane_digits)):
         hi, lo = split(block)
         hi_ref[16 * n : 16 * n + 16, :] = hi
-        if lo_ref is not None:
-            lo_ref[16 * n : 16 * n + 16, :] = lo
+        lo_ref[16 * n : 16 * n + 16, :] = lo
 
 
 def small_table(row_digits, lane_digits, mats):
@@ -138,22 +136,38 @@
     return n * (n + F32(1.0)) * F32(0.5)
 
 
-def table_a_kernel(ints, fl, pulse, w1h, w1l, w2h, w2l, wp, r1, r2, far, fai, o0):
-    w = 256
-    lane = iota((1, w), 1)
-    natural = [(lane >> 6) & 3, (lane >> 4) & 3, (lane >> 2) & 3, lane & 3]
-    moved = [
+def moved_lanes(lane):
+    return [
         (lane >> 3) & 3,
         (lane >> 1) & 3,
         (lane >> 6) & 3,
         ((lane >> 5) & 1) * 2 + (lane & 1),
     ]
+
+
+def lane_moves():
+    j1, j2, j3, j4 = moved_lanes(iota((1, 256), 1))
+    lanes = iota((256, 256), 0) == j1 * 64 + j2 * 16 + j3 * 4 + j4
+    return jnp.where(lanes, F32(1.0), F32(0.0)).astype(BF16)
+
+
+def row_moves(back):
+    n = iota((32, 32), 0 if back else 1)
+    m = iota((32, 32), 1 if back else 0)
+    rows = n == ((m >> 2) & 1) * 16 + (m & 3) * 4 + (m >> 3)
+    return jnp.where(rows, F32(1.0), F32(0.0)).astype(BF16)
+
+
+def table_a_kernel(ints, fl, pulse, x, w1h, w1l, w2h, w2l, r1, r2, far, fai, o0, gx, gr, gi):
+    w = 256
+    lane = iota((1, w), 1)
+    natural = [(lane >> 6) & 3, (lane >> 4) & 3, (lane >> 2) & 3, lane & 3]
+    moved = moved_lanes(lane)
     eye = identity(w)
     first = [rotation(ints, pulse, 0, k, w) for k in range(TRANSMONS)]
     second = {k: rotation(ints, pulse, 1, k, w) for k in (3, 4)}
     store_kron(w1h, w1l, [flip(first[k]) for k in (1, 2, 3, 4)], natural)
     store_kron(w2h, w2l, [eye, eye, flip(second[3]), flip(second[4])], moved)
-    store_kron(wp, None, [eye] * 4, moved)
     for a in range(4):
         for b in range(4):
             o0[4 * a + b : 4 * a + b + 1, :] = first[0][a][b]
@@ -177,8 +191,6 @@
     tables = [
         small_table(mov_r, nat_l, [one, one, g4]),
         small_table(nat_r, mov_l, [one, one, flip(g4)]),
-        small_table(mov_r, nat_l, [one, one, one]),
-        small_table(nat_r, mov_l, [one, one, one]),
     ]
     for n, t in enumerate(tables):
         hi, lo = split(t)
@@ -201,6 +213,26 @@
     sj, cj = sincos(aj)
     far[...] = mag * (ci * cj + si * sj)
     fai[...] = mag * (ci * sj - si * cj)
+    span = fnum(ints[2])
+    rd, cd = digits_a(ints)
+    (si, ci), (sj, cj) = factor_parts(fl, span, 1, F32(0.5) * span, rd, cd)
+    wide = [jnp.concatenate([d] * 8, axis=1) for d in rd]
+    mag = jnp.exp(F32(-0.5) * span * decay_of(fl, wide, cd))
+    si, ci = jnp.concatenate([si] * 8, axis=1), jnp.concatenate([ci] * 8, axis=1)
+    fr, fi = mag * (ci * cj + si * sj), mag * (ci * sj - si * cj)
+    gr[...] = fr
+    gi[...] = fi
+    re, im = x[0], x[1]
+    gx[0] = re * fr - im * fi
+    gx[1] = re * fi + im * fr
+
+
+def digits_a(ints):
+    row = ints[4] * 32 + iota((32, 128), 0)
+    col = iota((1, 1024), 1)
+    rd = [fnum((row >> (8 - 2 * k)) & 3) for k in range(TRANSMONS)]
+    cd = [fnum((col >> (8 - 2 * k)) & 3) for k in range(TRANSMONS)]
+    return rd, cd
 
 
 def start_of(ints, gathered):
@@ -246,18 +278,21 @@
     return total
 
 
-def first_factor(ints, fl, gathered):
-    span = fnum(ints[2])
-    time = start_of(ints, gathered) + F32(0.5) * span
-    row = ints[4] * 32 + iota((32, 128), 0)
-    col = iota((1, 1024), 1)
-    rd = [fnum((row >> (8 - 2 * k)) & 3) for k in range(TRANSMONS)]
-    cd = [fnum((col >> (8 - 2 * k)) & 3) for k in range(TRANSMONS)]
-    (si, ci), (sj, cj) = factor_parts(fl, span, 1, time, rd, cd)
-    wide = [jnp.concatenate([d] * 8, axis=1) for d in rd]
-    mag = jnp.exp(F32(-0.5) * span * decay_of(fl, wide, cd))
+def start_factor(ints, fl, gathered):
+    time = start_of(ints, gathered)
+    rd, cd = digits_a(ints)
+    phis = [drive_phase(fl, k, time) for k in range(TRANSMONS)]
+
+    def angle(digits):
+        total = phis[0] * drive_weight(digits[0])
+        for k in range(1, TRANSMONS):
+            total = total + phis[k] * drive_weight(digits[k])
+        return total
+
+    si, ci = sincos(angle(rd))
+    sj, cj = sincos(angle(cd))
     si, ci = jnp.concatenate([si] * 8, axis=1), jnp.concatenate([ci] * 8, axis=1)
-    return mag * (ci * cj + si * sj), mag * (ci * sj - si * cj)
+    return ci * cj + si * sj, ci * sj - si * cj
 
 
 def to_rows(blocks):
@@ -352,11 +387,17 @@
     return jnp.concatenate(out, axis=0)
 
 
+def raw_kernel(x, out):
+    blocks = to_rows(jnp.concatenate([x[0], x[1]], axis=1))
+    send(out, 0, pleft(row_moves(False), to_lanes(pmm(blocks, lane_moves()))))
+
+
 def forward_a_kernel(
-    ints, fl, gathered, x, f, w1h, w1l, w2h, w2l, wp, r1, r2, far, fai, o0, out
+    ints, fl, gathered, gx, other, w1h, w1l, w2h, w2l, r1, r2, far, fai, o0, out
 ):
-    fr, fi = first_factor(ints, fl, gathered)
-    re, im = x[0], x[1]
+    out[:, :, 256:] = other[...]
+    fr, fi = start_factor(ints, fl, gathered)
+    re, im = gx[0], gx[1]
     both = jnp.concatenate([re * fr - im * fi, re * fi + im * fr], axis=1)
     both = left(r1[0], r1[1], both)
     rows = mix_top(o0, to_rows(both), False)
@@ -364,12 +405,10 @@
     rows = apply_pointwise_a(rows, far[...], fai[...], False)
     rows = mm(rows, w2h[...], w2l[...])
     send(out, 0, left(r2[0], r2[1], to_lanes(rows)))
-    rows = to_rows(jnp.concatenate([f[0], f[1]], axis=1))
-    send(out, 256, pleft(r2[4], to_lanes(pmm(rows, wp[...]))))
 
 
 def adjoint_a_kernel(
-    ints, fl, gathered, y, m, w1h, w1l, w2h, w2l, wp, r1, r2, far, fai, o0, out
+    ints, fl, gathered, y, w1h, w1l, w2h, w2l, r1, r2, far, fai, o0, gr, gi, out
 ):
     rows = to_rows(left(r2[2], r2[3], receive(y, 0)))
     rows = mm(rows, w2h[...], w2l[...], True)
@@ -377,15 +416,22 @@
     rows = mm(rows, w1h[...], w1l[...], True)
     rows = mix_top(o0, rows, True)
     both = left(r1[2], r1[3], to_lanes(rows))
-    fr, fi = first_factor(ints, fl, gathered)
+    sr, si = start_factor(ints, fl, gathered)
+    fr, fi = gr[...] * sr - gi[...] * si, gr[...] * si + gi[...] * sr
     re, im = both[:, :1024], both[:, 1024:]
-    other = to_lanes(pmm(to_rows(pleft(r2[6], receive(m, 0))), wp[...], True))
-    out[0] = re * fr + im * fi - other[:, :1024]
-    out[1] = im * fr - re * fi - other[:, 1024:]
+    out[0] = re * fr + im * fi
+    out[1] = im * fr - re * fi
+
+
+def finish_kernel(x, m, out):
+    rows = to_rows(pleft(row_moves(True), receive(m, 0)))
+    other = to_lanes(pmm(rows, lane_moves(), True))
+    out[0] = x[0] - other[:, :1024]
+    out[1] = x[1] - other[:, 1024:]
 
 
 def table_b_kernel(
-    ints, fl, gathered, pulse, a1h, a1l, b1h, b1l, a2h, a2l, b2h, b2l, vh, vl, fmr, fmi, ffr, ffi
+    ints, fl, pulse, gathered, a1h, a1l, b1h, b1l, a2h, a2l, b2h, b2l, vh, vl, fmr, fmi, ffr, ffi
 ):
     w = 256
     lane = iota((1, w), 1)
@@ -474,10 +520,19 @@
 VMEM = pl.BlockSpec(memory_space=pltpu.VMEM)
 
 
+def with_params(kernel):
+    def run(segment, tick, rank, shift, coupling, dephase, detuning, *refs):
+        ints = [segment[0, 0], segment[0, 1], tick[0, 0], tick[0, 1], rank[0], rank[1]]
+        sources = ((shift, 5), (coupling, 4), (dephase, 5), (detuning, 5))
+        kernel(ints, [ref[n] for ref, count in sources for n in range(count)], *refs)
+
+    return run
+
+
 def call(kernel, args, scalars, outs, flops, name):
-    specs = [SMEM if n in scalars else VMEM for n in range(len(args))]
+    specs = [SMEM if n < scalars else VMEM for n in range(len(args))]
     return pl.pallas_call(
-        kernel,
+        with_params(kernel) if scalars else kernel,
         in_specs=specs,
         out_specs=jax.tree.map(lambda _: VMEM, outs),
         out_shape=outs,
@@ -494,76 +549,76 @@
 def local(linkage, pulse, segments, ticks, detuning, level_shift, coupling, dephase):
     current = linkage[:, 0]
     phases = lax.axis_size("phase")
-    ints = jnp.concatenate(
-        [
-            segments[0],
-            ticks[0],
-            jnp.stack([lax.axis_index("row"), lax.axis_index("phase")]).astype(jnp.int32),
-        ]
-    )
-    floats = jnp.concatenate([level_shift, coupling, dephase, detuning])
-    flat_pulse = pulse.reshape(-1)
+    rank = jnp.stack([lax.axis_index("row"), lax.axis_index("phase")]).astype(jnp.int32)
+    params = (segments, ticks, rank, level_shift, coupling, dephase, detuning)
+    angles = jnp.transpose(pulse, (1, 2, 0))
     gathered = lax.all_to_all(
         jnp.broadcast_to(ticks, (phases, STEPS)), "phase", split_axis=0, concat_axis=0, tiled=True
     )
-    following = lax.ppermute(
-        current, "phase", [((i + 1) % phases, i) for i in range(phases)]
-    )
+    def turn(x):
+        return lax.all_to_all(
+            x.reshape(32, 8, 512), "row", split_axis=0, concat_axis=0, tiled=True
+        )
+
+    following = lax.ppermute(current, "phase", [((i + 1) % phases, i) for i in range(phases)])
+    following = call(raw_kernel, (following,), 0, sds(32, 8, 256), 1 << 26, "raw")
     square = sds(256, 256, dtype=BF16)
-    tables_a = call(
+    *tables_a, weighed, gr, gi = call(
         table_a_kernel,
-        (ints, floats, flat_pulse),
-        (0, 1, 2),
+        (*params, angles, current),
+        8,
         (
-            *([square] * 5),
+            *([square] * 4),
             sds(4, 32, 32, dtype=BF16),
-            sds(8, 32, 32, dtype=BF16),
+            sds(4, 32, 32, dtype=BF16),
             sds(32, 128),
             sds(32, 128),
             sds(16, 256),
+            sds(2, 32, 1024),
+            sds(32, 1024),
+            sds(32, 1024),
         ),
         1 << 28,
         "table_a",
     )
     sent = call(
         forward_a_kernel,
-        (ints, floats, gathered, current, following, *tables_a),
-        (0, 1),
+        (*params, gathered, weighed, following, *tables_a),
+        7,
         sds(32, 8, 512),
         1 << 28,
         "forward_a",
     )
-    turned = lax.all_to_all(sent, "row", split_axis=0, concat_axis=0, tiled=True)
+    turned = turn(sent)
     tables_b = call(
         table_b_kernel,
-        (ints, floats, gathered, flat_pulse),
-        (0, 1, 3),
+        (*params, angles, gathered),
+        8,
         (*([square] * 10), *([sds(256, 128)] * 4)),
-        1 << 30,
+        1 << 28,
         "table_b",
     )
     back = call(
         both_b_kernel,
         (turned.reshape(256, 512), *tables_b),
-        (),
+        0,
         sds(256, 512),
         1 << 28,
         "both_b",
     )
-    returned = lax.all_to_all(
-        back.reshape(32, 8, 512), "row", split_axis=0, concat_axis=0, tiled=True
-    )
+    returned = turn(back)
     earlier = lax.ppermute(
         returned[:, :, 256:], "phase", [(i, (i + 1) % phases) for i in range(phases)]
     )
-    result = call(
+    costate = call(
         adjoint_a_kernel,
-        (ints, floats, gathered, returned, earlier, *tables_a),
-        (0, 1),
+        (*params, gathered, returned, *tables_a, gr, gi),
+        7,
         sds(2, 32, 1024),
         1 << 28,
         "adjoint_a",
     )
+    result = call(finish_kernel, (costate, earlier), 0, sds(2, 32, 1024), 1 << 26, "finish")
     return result[:, None]
 
 

time: 77 us -> 74.8 us (0.971)
  waiting for transfers between devices: 24.3 us -> 21 us
  Pallas kernels: 11.4 us -> 12.6 us
    ppermute x1, waiting for transfers between devices: 6.99 us -> 5.01 us  [local(): lax.ppermute(returned[:, :, 256:], 'phase', [(i, (i + 1) % phases) for i...]
    pallas_call x5 -> x7, Pallas kernels: 11.4 us -> 12.6 us  [call(): pl.pallas_call(with_params(kernel) if scalars else kernel, in_specs=specs...]
    all_to_all x1, waiting for transfers between devices: 2.32 us -> 1.14 us  [local(): lax.all_to_all(jnp.broadcast_to(ticks, (phases, STEPS)), 'phase', split_a...]
    unnamed x17 -> x16, local copies, waits for them, and re-layouts: 1.41 us -> 1.65 us
  transfers between devices with their start and end apart: 4 -> 4, of which waited for: 3 -> 3; matrix products, arithmetic and copies ran while one was open for 1% -> 1% of each run, Pallas kernels for 4% -> 9%
where the time goes in v2:
time: 74.8 us; the launch traced here: 74.4 us
  blocking collectives  21.4 us (29%)
  waiting for transfers between devices  21 us (28%)
  starting transfers between devices  17 us (23%)
  Pallas kernels  12.6 us (17%)
  local copies, waits for them, and re-layouts  2.26 us (3%)
    all_to_all x1, blocking collectives, turn(): lax.all_to_all(x.reshape(32, 8, 512), 'row', split_axis=0, concat_axis=0,...  21.4 us
    all_to_all x1, waiting for transfers between devices, turn(): lax.all_to_all(x.reshape(32, 8, 512), 'row', split_axis=0, concat_axis=0,...  14.8 us
    pallas_call x7, Pallas kernels, call(): pl.pallas_call(with_params(kernel) if scalars else kernel, in_specs=specs...  12.6 us
    all_to_all x1, starting transfers between devices, turn(): lax.all_to_all(x.reshape(32, 8, 512), 'row', split_axis=0, concat_axis=0,...  11.2 us
    ppermute x1, waiting for transfers between devices, local(): lax.ppermute(returned[:, :, 256:], 'phase', [(i, (i + 1) % phases) for i...  5.01 us
    all_to_all x1, starting transfers between devices, local(): lax.all_to_all(jnp.broadcast_to(ticks, (phases, STEPS)), 'phase', split_a...  3.31 us
    ppermute x1, starting transfers between devices, local(): lax.ppermute(current, 'phase', [((i + 1) % phases, i) for i in range(phas...  2.45 us
    unnamed x16, local copies, waits for them, and re-layouts  1.65 us
  transfers between devices with their start and end apart: 4, of which 3 were waited for; matrix products, arithmetic and copies ran while one was open for 1% of the time, Pallas kernels for 9%

profile of v2, /device:TPU:32, one launch (start us, length us, event | category | flops | bytes accessed | tf_op | source)
XLA Modules:
  0.0 74.4 jit_solution(12286828346752570167)
XLA Ops:
  0.0 0.0 copy-start
  0.0 2.5 %collective-permute-start = (f32[2,32,1024]{2,1,0:T(8,128)}, f32[2,32,1024]{2,1,0:T(8,128)S(1)}, u32[]{:S(2)}, u32[]{:S(2)}) collective-permute-start(f32[2,32,1024]{2,1,0:T(8,128)} %bitcast.17), channel_id=1, source_target_pairs={{32,0},{64,32},{96,64},{128,96},{160,128},{192,160},{224,192},{0,2... | collective-permute-start | bytes 786440 | tf_op jit(solution)/shard_map/ppermute | solution.py:563
  2.5 0.0 copy-done
  2.5 0.6 broadcast_in_dim.8
  3.1 3.3 %all-to-all-start = ((s32[8,1,2]{2,1,0:T(1,128)}), s32[8,1,2]{2,1,0:T(1,128)S(1)}, u32[]{:S(2)}, u32[]{:S(2)}) async-start(s32[8,1,2]{2,1,0:T(1,128)} %broadcast_in_dim.8), calls=%async_computation | async-start | bytes 8192 | tf_op jit(solution)/shard_map/all_to_all | solution.py:555
  6.4 0.0 copy-start.7
  6.4 0.0 copy-start.4
  6.4 0.0 copy-start.5
  6.4 0.1 pad_add_fusion.rank
  6.5 0.0 copy-start.1
  6.5 0.0 copy-start.2
  6.5 0.0 copy-start.3
  6.5 0.6 copy-done.7
  7.1 0.0 copy-done.4
  7.1 0.0 copy-done.5
  7.1 0.1 copy-done.1
  7.1 0.0 copy-done.2
  7.2 0.0 copy-done.3
  7.2 0.0 copy-start.6
  7.2 0.9 %copy-done.6 = f32[2,1,32,1024]{3,2,1,0:T(8,128)S(1)} copy-done((f32[2,1,32,1024]{3,2,1,0:T(8,128)S(1)}, f32[2,1,32,1024]{3,2,1,0:T(8,128)}, u32[]{:S(2)}) %copy-start.6) | copy-done | bytes 262168
  8.1 1.5 %table_a.1 = (bf16[256,256]{1,0:T(8,128)(2,1)S(1)}, bf16[256,256]{1,0:T(8,128)(2,1)S(1)}, bf16[256,256]{1,0:T(8,128)(2,1)S(1)}, bf16[256,256]{1,0:T(8,128)(2,1)S...) custom-call(s32[1,2]{1,0:T(1,128)S(1)} %copy-done.1, ...), custom_call_target="tpu_custom_call" | custom-call | flops 268435456 | bytes 1048576 | tf_op jit(solution)/shard_map/table_a/pallas_call | solution.py:534
  9.6 0.0 collective-permute-done.x
  9.6 0.7 raw.1.refs_2_
  10.4 1.1 %all-to-all-done = s32[8,1,2]{2,1,0:T(1,128)S(1)} async-done(((s32[8,1,2]{2,1,0:T(1,128)}), s32[8,1,2]{2,1,0:T(1,128)S(1)}, u32[]{:S(2)}, u32[]{:S(2)}) %all-to-all-start) | async-done | bytes 96 | tf_op jit(solution)/shard_map/all_to_all | solution.py:555
  11.5 2.9 %forward_a.1 = f32[32,8,512]{2,1,0:T(8,128)} custom-call(s32[1,2]{1,0:T(1,128)S(1)} %copy-done.1, s32[1,2]{1,0:T(1,128)S(1)} %copy-done, s32[2]{0:T(128)S(1)} %pad_add_fusion.rank, f32[5]{0:T(128)S(1)} %copy-done.2, f32[4]{0:T(128)S(1)} %copy-done.3, f32[5]{0:T(128)S(1)} %copy-done.4, f32[5]{0:T(128)S(1)} %copy-done.5, s32[8,2]{1,0:T(8,128)S(1)} %bitcast.13, ...), custom_call_target="tpu_custom_call" | custom-call | flops 268435456 | bytes 1048576 | tf_op jit(solution)/shard_map/forward_a/pallas_call | solution.py:534
  14.4 11.2 %all-to-all-start.1 = ((f32[32,8,512]{2,1,0:T(8,128)}), f32[32,8,512]{2,1,0:T(8,128)S(1)}, u32[]{:S(2)}, u32[]{:S(2)}) async-start(f32[32,8,512]{2,1,0:T(8,128)} %forward_a.1), calls=%async_computation.1 | async-start | bytes 1048576 | tf_op jit(solution)/shard_map/all_to_all | solution.py:559
  25.6 2.3 %table_b.1 = (bf16[256,256]{1,0:T(8,128)(2,1)S(1)}, bf16[256,256]{1,0:T(8,128)(2,1)S(1)}, bf16[256,256]{1,0:T(8,128)(2,1)S(1)}, bf16[256,256]{1,0:T(8,128)(2,1)S...) custom-call(s32[1,2]{1,0:T(1,128)S(1)} %copy-done.1, ...), custom_call_target="tpu_custom_call" | custom-call | flops 268435456 | bytes 1048576 | tf_op jit(solution)/shard_map/table_b/pallas_call | solution.py:534
  27.9 14.8 %all-to-all-done.1 = f32[32,8,512]{2,1,0:T(8,128)S(1)} async-done(((f32[32,8,512]{2,1,0:T(8,128)}), f32[32,8,512]{2,1,0:T(8,128)S(1)}, u32[]{:S(2)}, u32[]{:S(2)}) %all-to-all-start.1) | async-done | bytes 524320 | tf_op jit(solution)/shard_map/all_to_all | solution.py:559
  42.8 1.8 %both_b.1 = f32[256,512]{1,0:T(8,128)S(1)} custom-call(f32[256,512]{1,0:T(8,128)S(1)} %bitcast.11, bf16[256,256]{1,0:T(8,128)(2,1)S(1)} %get-tuple-element.41.a1h, bf16[256,256]{1,0:T(8,128)(2,1)S(1)} %get-tuple-element.42.a1l, bf16[256,256]{1,0:T(8,128)(2,1)S(1)} %get-tuple-element.43.b1h, bf16[256,256]{1,0:T(8,128)(2,1)S(1)} %get-tuple-element.44.b1l, ...), custom_call_target="tpu_custom_call" | custom-call | flops 268435456 | bytes 1048576 | tf_op jit(solution)/shard_map/both_b/pallas_call | solution.py:534
  44.6 21.4 %all_to_all.18.refs_1_ = f32[32,8,512]{2,1,0:T(8,128)S(1)} all-to-all(f32[32,8,512]{2,1,0:T(8,128)S(1)} %bitcast.12), channel_id=1, replica_groups=mesh['phase'=8,'row'=32] {'row'}, dimensions={0} | all-to-all | bytes 1048576 | tf_op jit(solution)/shard_map/all_to_all | solution.py:559
  66.1 0.0 collective-permute-start.1
  66.1 2.0 %adjoint_a.1.x = f32[2,32,1024]{2,1,0:T(8,128)S(1)} custom-call(s32[1,2]{1,0:T(1,128)S(1)} %copy-done.1, s32[1,2]{1,0:T(1,128)S(1)} %copy-done, s32[2]{0:T(128)S(1)} %pad_add_fusion.rank, f32[5]{0:T(128)S(1)} %copy-done.2, f32[4]{0:T(128)S(1)} %copy-done.3, f32[5]{0:T(128)S(1)} %copy-done.4, f32[5]{0:T(128)S(1)} %copy-done.5, s32[8,2]{1,0:T(8,128)S(1)} %bitcast.15, ...), custom_call_target="tpu_custom_call" | custom-call | flops 268435456 | bytes 1048576 | tf_op jit(solution)/shard_map/adjoint_a/pallas_call | solution.py:534
  68.1 5.0 %collective-permute-done.1.m = f32[32,8,256]{2,1,0:T(8,128)S(1)} collective-permute-done((f32[32,8,256]{2,1,0:T(8,128)S(1)}, f32[32,8,256]{2,1,0:T(8,128)S(1)}, u32[]{:S(2)}, u32[]{:S(2)}) %collective-permute-start.1) | collective-permute-done | bytes 262176 | tf_op jit(solution)/shard_map/ppermute | solution.py:610
  73.1 1.3 %finish.1 = f32[2,32,1024]{2,1,0:T(8,128)} custom-call(f32[2,32,1024]{2,1,0:T(8,128)S(1)} %adjoint_a.1.x, f32[32,8,256]{2,1,0:T(8,128)S(1)} %collective-permute-done.1.m), custom_call_target="tpu_custom_call" | custom-call | flops 67108864 | bytes 1048576 | tf_op jit(solution)/shard_map/finish/pallas_call | solution.py:534
  (1 shorter events, 0.0 us)
Async XLA Ops:
  0.0 2.5 %copy-start = (s32[1,2]{1,0:T(1,128)S(1)}, s32[1,2]{1,0:T(1,128)}, u32[]{:S(2)}) copy-start(s32[1,2]{1,0:T(1,128)} %tick.7) | copy-start | bytes 28
  0.0 9.6 %collective-permute-start = (f32[2,32,1024]{2,1,0:T(8,128)}, f32[2,32,1024]{2,1,0:T(8,128)S(1)}, u32[]{:S(2)}, u32[]{:S(2)}) collective-permute-start(f32[2,32,1024]{2,1,0:T(8,128)} %bitcast.17), channel_id=1, source_target_pairs={{32,0},{64,32},{96,64},{128,96},{160,128},{192,160},{224,192},{0,2... | collective-permute-start | bytes 786440 | tf_op jit(solution)/shard_map/ppermute | solution.py:563
  3.1 8.5 %all-to-all-start = ((s32[8,1,2]{2,1,0:T(1,128)}), s32[8,1,2]{2,1,0:T(1,128)S(1)}, u32[]{:S(2)}, u32[]{:S(2)}) async-start(s32[8,1,2]{2,1,0:T(1,128)} %broadcast_in_dim.8), calls=%async_computation | async-start | bytes 8192 | tf_op jit(solution)/shard_map/all_to_all | solution.py:555
  6.4 0.7 copy-start.7
  6.4 0.7 copy-start.4
  6.4 0.7 copy-start.5
  6.5 0.7 copy-start.1
  6.5 0.7 copy-start.2
  6.5 0.7 copy-start.3
  7.2 0.9 %copy-start.6 = (f32[2,1,32,1024]{3,2,1,0:T(8,128)S(1)}, f32[2,1,32,1024]{3,2,1,0:T(8,128)}, u32[]{:S(2)}) copy-start(f32[2,1,32,1024]{3,2,1,0:T(8,128)} %param.8) | copy-start | bytes 786436
  14.4 28.4 %all-to-all-start.1 = ((f32[32,8,512]{2,1,0:T(8,128)}), f32[32,8,512]{2,1,0:T(8,128)S(1)}, u32[]{:S(2)}, u32[]{:S(2)}) async-start(f32[32,8,512]{2,1,0:T(8,128)} %forward_a.1), calls=%async_computation.1 | async-start | bytes 1048576 | tf_op jit(solution)/shard_map/all_to_all | solution.py:559
  66.1 7.0 %collective-permute-start.1 = (f32[32,8,256]{2,1,0:T(8,128)S(1)}, f32[32,8,256]{2,1,0:T(8,128)S(1)}, u32[]{:S(2)}, u32[]{:S(2)}) collective-permute-start(f32[32,8,256]{2,1,0:T(8,128)S(1)} %slice.4), channel_id=1, source_target_pairs={{0,32},{32,64},{64,96},{96,128},{128,160},{160,192},{192,224},{224... | collective-permute-start | bytes 786440 | tf_op jit(solution)/shard_map/ppermute | solution.py:610

commit v3 on v2

--- a/solution.py
+++ b/solution.py
@@ -116,14 +116,6 @@
         lo_ref[16 * n : 16 * n + 16, :] = lo
 
 
-def small_table(row_digits, lane_digits, mats):
-    out = None
-    for o, rd, ld in zip(mats, row_digits, lane_digits):
-        part = pick(rd, lane_rows(o, ld))
-        out = part if out is None else out * part
-    return out
-
-
 def fnum(x):
     return x.astype(F32)
 
@@ -151,14 +143,39 @@
     return jnp.where(lanes, F32(1.0), F32(0.0)).astype(BF16)
 
 
+def moved_row(m):
+    return (m & ~31) + ((m >> 2) & 1) * 16 + (m & 3) * 4 + ((m >> 3) & 3)
+
+
 def row_moves(back):
-    n = iota((32, 32), 0 if back else 1)
-    m = iota((32, 32), 1 if back else 0)
-    rows = n == ((m >> 2) & 1) * 16 + (m & 3) * 4 + (m >> 3)
+    if back:
+        rows = iota((256, 256), 0) == moved_row(iota((1, 256), 1))
+    else:
+        rows = moved_row(iota((256, 1), 0)) == iota((256, 256), 1)
     return jnp.where(rows, F32(1.0), F32(0.0)).astype(BF16)
 
 
-def table_a_kernel(ints, fl, pulse, x, w1h, w1l, w2h, w2l, r1, r2, far, fai, o0, gx, gr, gi):
+def store_rows_a(hi_ref, lo_ref, o0, o3, o4):
+    lane = iota((1, 256), 1)
+    row = iota((16, 256), 0)
+    t0, t3, t4 = (
+        lane_rows(o, d) for o, d in ((o0, (lane >> 6) & 3), (o3, (lane >> 2) & 3), (o4, lane & 3))
+    )
+    same = ((row >> 2) & 1) == ((lane >> 4) & 1)
+    low = pick(row & 3, t3) * jnp.where(same, F32(1.0), F32(0.0))
+    mid = [low * jnp.where((row >> 3) == 0, t4[2 * h], t4[2 * h + 1]) for h in range(2)]
+    for n in range(16):
+        kept = jnp.where(((lane >> 5) & 1) == ((n >> 1) & 1), F32(1.0), F32(0.0))
+        hi, lo = split(mid[n & 1] * (t0[n >> 2] * kept))
+        hi_ref[16 * n : 16 * n + 16, :] = hi
+        lo_ref[16 * n : 16 * n + 16, :] = lo
+
+
+def table_a_kernel(
+    ints, fl, pulse, source, w1h, w1l, w2h, w2l, k1h, k1l, far, fai, o4, gx, x, sem
+):
+    fetch = pltpu.make_async_copy(source, x, sem)
+    fetch.start()
     w = 256
     lane = iota((1, w), 1)
     natural = [(lane >> 6) & 3, (lane >> 4) & 3, (lane >> 2) & 3, lane & 3]
@@ -168,37 +185,14 @@
     second = {k: rotation(ints, pulse, 1, k, w) for k in (3, 4)}
     store_kron(w1h, w1l, [flip(first[k]) for k in (1, 2, 3, 4)], natural)
     store_kron(w2h, w2l, [eye, eye, flip(second[3]), flip(second[4])], moved)
+    store_rows_a(k1h, k1l, first[0], first[3], first[4])
     for a in range(4):
         for b in range(4):
-            o0[4 * a + b : 4 * a + b + 1, :] = first[0][a][b]
-    rl = iota((1, 32), 1)
-    rr = iota((32, 32), 0)
-    one = [[e[:, :32] for e in row] for row in eye]
-    f3 = [[e[:, :32] for e in row] for row in first[3]]
-    f4 = [[e[:, :32] for e in row] for row in first[4]]
-    g4 = [[e[:, :32] for e in row] for row in second[4]]
-    nat_r = [rr >> 4, (rr >> 2) & 3, rr & 3]
-    nat_l = [rl >> 4, (rl >> 2) & 3, rl & 3]
-    mov_r = [(rr >> 2) & 1, rr & 3, rr >> 3]
-    mov_l = [(rl >> 2) & 1, rl & 3, rl >> 3]
-    tables = [
-        small_table(nat_r, nat_l, [one, f3, f4]),
-        small_table(nat_r, nat_l, [one, flip(f3), flip(f4)]),
-    ]
-    for n, t in enumerate(tables):
-        hi, lo = split(t)
-        r1[2 * n], r1[2 * n + 1] = hi, lo
-    tables = [
-        small_table(mov_r, nat_l, [one, one, g4]),
-        small_table(nat_r, mov_l, [one, one, flip(g4)]),
-    ]
-    for n, t in enumerate(tables):
-        hi, lo = split(t)
-        r2[2 * n], r2[2 * n + 1] = hi, lo
+            o4[4 * a + b : 4 * a + b + 1, :] = second[4][a][b]
     t12 = F32(0.5) * (fnum(ints[2]) + fnum(ints[3]))
     row = iota((32, 128), 0)
     col = iota((1, 128), 1)
-    i3, i4 = fnum((row >> 2) & 3), fnum(row & 3)
+    i3, i4 = fnum(row & 3), fnum(row >> 3)
     j2, j3, j4 = fnum((col >> 4) & 3), fnum((col >> 2) & 3), fnum(col & 3)
 
     def node(k, n):
@@ -213,18 +207,21 @@
     sj, cj = sincos(aj)
     far[...] = mag * (ci * cj + si * sj)
     fai[...] = mag * (ci * sj - si * cj)
+    fr, fi = first_factor(ints, fl, F32(0.5) * fnum(ints[2]))
+    fetch.wait()
+    re, im = x[0], x[1]
+    gx[0] = re * fr - im * fi
+    gx[1] = re * fi + im * fr
+
+
+def first_factor(ints, fl, time):
     span = fnum(ints[2])
     rd, cd = digits_a(ints)
-    (si, ci), (sj, cj) = factor_parts(fl, span, 1, F32(0.5) * span, rd, cd)
+    (si, ci), (sj, cj) = factor_parts(fl, span, 1, time, rd, cd)
     wide = [jnp.concatenate([d] * 8, axis=1) for d in rd]
     mag = jnp.exp(F32(-0.5) * span * decay_of(fl, wide, cd))
     si, ci = jnp.concatenate([si] * 8, axis=1), jnp.concatenate([ci] * 8, axis=1)
-    fr, fi = mag * (ci * cj + si * sj), mag * (ci * sj - si * cj)
-    gr[...] = fr
-    gi[...] = fi
-    re, im = x[0], x[1]
-    gx[0] = re * fr - im * fi
-    gx[1] = re * fi + im * fr
+    return mag * (ci * cj + si * sj), mag * (ci * sj - si * cj)
 
 
 def digits_a(ints):
@@ -313,16 +310,22 @@
     )
 
 
-def mix_top(o0, rows, transposed):
+def mix_i4(o4, rows, transposed):
+    parts = [
+        jnp.concatenate([rows[32 * n + 8 * b : 32 * n + 8 * b + 8, :] for n in range(8)], axis=0)
+        for b in range(4)
+    ]
     out = []
     for a in range(4):
         total = None
         for b in range(4):
             n = 4 * b + a if transposed else 4 * a + b
-            part = rows[64 * b : 64 * b + 64, :] * o0[n : n + 1, :]
+            part = parts[b] * o4[n : n + 1, :]
             total = part if total is None else total + part
         out.append(total)
-    return jnp.concatenate(out, axis=0)
+    return jnp.concatenate(
+        [out[a][8 * n : 8 * n + 8, :] for n in range(8) for a in range(4)], axis=0
+    )
 
 
 def chunk_of_lane(shape):
@@ -388,44 +391,47 @@
 
 
 def raw_kernel(x, out):
-    blocks = to_rows(jnp.concatenate([x[0], x[1]], axis=1))
-    send(out, 0, pleft(row_moves(False), to_lanes(pmm(blocks, lane_moves()))))
+    rows = to_rows(jnp.concatenate([x[0], x[1]], axis=1))
+    send(out, 0, to_lanes(pmm(pleft(row_moves(False), rows), lane_moves())))
 
 
 def forward_a_kernel(
-    ints, fl, gathered, gx, other, w1h, w1l, w2h, w2l, r1, r2, far, fai, o0, out
+    ints, fl, gathered, gx, other, w1h, w1l, w2h, w2l, k1h, k1l, far, fai, o4, out
 ):
     out[:, :, 256:] = other[...]
     fr, fi = start_factor(ints, fl, gathered)
     re, im = gx[0], gx[1]
-    both = jnp.concatenate([re * fr - im * fi, re * fi + im * fr], axis=1)
-    both = left(r1[0], r1[1], both)
-    rows = mix_top(o0, to_rows(both), False)
-    rows = mm(rows, w1h[...], w1l[...])
+    rows = to_rows(jnp.concatenate([re * fr - im * fi, re * fi + im * fr], axis=1))
+    rows = mm(left(k1h[...], k1l[...], rows), w1h[...], w1l[...])
     rows = apply_pointwise_a(rows, far[...], fai[...], False)
-    rows = mm(rows, w2h[...], w2l[...])
-    send(out, 0, left(r2[0], r2[1], to_lanes(rows)))
+    send(out, 0, to_lanes(mm(mix_i4(o4, rows, False), w2h[...], w2l[...])))
 
 
 def adjoint_a_kernel(
-    ints, fl, gathered, y, w1h, w1l, w2h, w2l, r1, r2, far, fai, o0, gr, gi, out
+    ints, fl, pulse, gathered, y, w1h, w1l, w2h, w2l, far, fai, o4, out, t1h, t1l
 ):
-    rows = to_rows(left(r2[2], r2[3], receive(y, 0)))
-    rows = mm(rows, w2h[...], w2l[...], True)
-    rows = apply_pointwise_a(rows, far[...], fai[...], True)
+    rows = mm(to_rows(receive(y, 0)), w2h[...], w2l[...], True)
+    rows = apply_pointwise_a(mix_i4(o4, rows, True), far[...], fai[...], True)
     rows = mm(rows, w1h[...], w1l[...], True)
-    rows = mix_top(o0, rows, True)
-    both = left(r1[2], r1[3], to_lanes(rows))
-    sr, si = start_factor(ints, fl, gathered)
-    fr, fi = gr[...] * sr - gi[...] * si, gr[...] * si + gi[...] * sr
+    lane = iota((1, 256), 1)
+    sent = [
+        (lane >> 6) & 3,
+        ((lane >> 5) & 1) * 2 + ((lane >> 2) & 1),
+        lane & 3,
+        (lane >> 3) & 3,
+    ]
+    first = [flip(rotation(ints, pulse, 0, k, 256)) for k in (0, 3, 4)]
+    store_kron(t1h, t1l, [first[0], identity(256), first[1], first[2]], sent)
+    both = to_lanes(left(t1h[...], t1l[...], rows))
+    fr, fi = first_factor(ints, fl, start_of(ints, gathered) + F32(0.5) * fnum(ints[2]))
     re, im = both[:, :1024], both[:, 1024:]
     out[0] = re * fr + im * fi
     out[1] = im * fr - re * fi
 
 
 def finish_kernel(x, m, out):
-    rows = to_rows(pleft(row_moves(True), receive(m, 0)))
-    other = to_lanes(pmm(rows, lane_moves(), True))
+    rows = pmm(to_rows(receive(m, 0)), lane_moves(), True)
+    other = to_lanes(pleft(row_moves(True), rows))
     out[0] = x[0] - other[:, :1024]
     out[1] = x[1] - other[:, 1024:]
 
@@ -518,6 +524,7 @@
 
 SMEM = pl.BlockSpec(memory_space=pltpu.SMEM)
 VMEM = pl.BlockSpec(memory_space=pltpu.VMEM)
+HBM = pl.BlockSpec(memory_space=pltpu.MemorySpace.HBM)
 
 
 def with_params(kernel):
@@ -529,13 +536,14 @@
     return run
 
 
-def call(kernel, args, scalars, outs, flops, name):
-    specs = [SMEM if n < scalars else VMEM for n in range(len(args))]
+def call(kernel, args, scalars, outs, flops, name, far=(), scratch=()):
+    specs = [SMEM if n < scalars else HBM if n in far else VMEM for n in range(len(args))]
     return pl.pallas_call(
         with_params(kernel) if scalars else kernel,
         in_specs=specs,
         out_specs=jax.tree.map(lambda _: VMEM, outs),
         out_shape=outs,
+        scratch_shapes=scratch,
         name=name,
         compiler_params=pltpu.CompilerParams(vmem_limit_bytes=16 << 20),
         cost_estimate=pl.CostEstimate(flops=flops, transcendentals=0, bytes_accessed=1 << 20),
@@ -563,23 +571,25 @@
     following = lax.ppermute(current, "phase", [((i + 1) % phases, i) for i in range(phases)])
     following = call(raw_kernel, (following,), 0, sds(32, 8, 256), 1 << 26, "raw")
     square = sds(256, 256, dtype=BF16)
-    *tables_a, weighed, gr, gi = call(
+    *tables_a, weighed = call(
         table_a_kernel,
-        (*params, angles, current),
+        (
+            *params,
+            angles,
+            pltpu.with_memory_space_constraint(current, pltpu.MemorySpace.HBM),
+        ),
         8,
         (
-            *([square] * 4),
-            sds(4, 32, 32, dtype=BF16),
-            sds(4, 32, 32, dtype=BF16),
+            *([square] * 6),
             sds(32, 128),
             sds(32, 128),
             sds(16, 256),
             sds(2, 32, 1024),
-            sds(32, 1024),
-            sds(32, 1024),
         ),
         1 << 28,
         "table_a",
+        far=(8,),
+        scratch=(pltpu.VMEM((2, 32, 1024), F32), pltpu.SemaphoreType.DMA),
     )
     sent = call(
         forward_a_kernel,
@@ -612,11 +622,12 @@
     )
     costate = call(
         adjoint_a_kernel,
-        (*params, gathered, returned, *tables_a, gr, gi),
-        7,
+        (*params, angles, gathered, returned, *tables_a[:4], *tables_a[6:]),
+        8,
         sds(2, 32, 1024),
         1 << 28,
         "adjoint_a",
+        scratch=(pltpu.VMEM((256, 256), BF16), pltpu.VMEM((256, 256), BF16)),
     )
     result = call(finish_kernel, (costate, earlier), 0, sds(2, 32, 1024), 1 << 26, "finish")
     return result[:, None]

time: 74.8 us -> 74.7 us (level)
  local copies, waits for them, and re-layouts: 2.26 us -> 1.31 us
    unnamed x16 -> x14, local copies, waits for them, and re-layouts: 1.65 us -> 0.7 us
where the time goes in v3:
time: 74.7 us; the launch traced here: 74.3 us
  waiting for transfers between devices  21.6 us (29%)
  blocking collectives  21.4 us (29%)
  starting transfers between devices  17 us (23%)
  Pallas kernels  12.8 us (17%)
  local copies, waits for them, and re-layouts  1.31 us (2%)
    all_to_all x1, blocking collectives, turn(): lax.all_to_all(x.reshape(32, 8, 512), 'row', split_axis=0, concat_axis=0,...  21.4 us
    all_to_all x1, waiting for transfers between devices, turn(): lax.all_to_all(x.reshape(32, 8, 512), 'row', split_axis=0, concat_axis=0,...  14.8 us
    pallas_call x7, Pallas kernels, call(): pl.pallas_call(with_params(kernel) if scalars else kernel, in_specs=specs...  12.8 us
    all_to_all x1, starting transfers between devices, turn(): lax.all_to_all(x.reshape(32, 8, 512), 'row', split_axis=0, concat_axis=0,...  11.2 us
    ppermute x1, waiting for transfers between devices, local(): lax.ppermute(returned[:, :, 256:], 'phase', [(i, (i + 1) % phases) for i...  4.92 us
    all_to_all x1, starting transfers between devices, local(): lax.all_to_all(jnp.broadcast_to(ticks, (phases, STEPS)), 'phase', split_a...  3.31 us
    ppermute x1, starting transfers between devices, local(): lax.ppermute(current, 'phase', [((i + 1) % phases, i) for i in range(phas...  2.45 us
    all_to_all x1, waiting for transfers between devices, local(): lax.all_to_all(jnp.broadcast_to(ticks, (phases, STEPS)), 'phase', split_a...  1.86 us
  transfers between devices with their start and end apart: 4, of which 3 were waited for; matrix products, arithmetic and copies ran while one was open for 1% of the time, Pallas kernels for 9%

profile of v3, /device:TPU:32, one launch (start us, length us, event | category | flops | bytes accessed | tf_op | source)
XLA Modules:
  0.0 74.3 jit_solution(6180037050984729669)
XLA Ops:
  0.0 0.0 copy-start.1
  0.0 2.5 %collective-permute-start = (f32[2,32,1024]{2,1,0:T(8,128)}, f32[2,32,1024]{2,1,0:T(8,128)S(1)}, u32[]{:S(2)}, u32[]{:S(2)}) collective-permute-start(f32[2,32,1024]{2,1,0:T(8,128)} %bitcast.20), channel_id=1, source_target_pairs={{32,0},{64,32},{96,64},{128,96},{160,128},{192,160},{224,192},{0,2... | collective-permute-start | bytes 786440 | tf_op jit(solution)/shard_map/ppermute | solution.py:571
  2.5 0.0 copy-done.1
  2.5 0.6 broadcast_in_dim.8
  3.1 3.3 %all-to-all-start = ((s32[8,1,2]{2,1,0:T(1,128)}), s32[8,1,2]{2,1,0:T(1,128)S(1)}, u32[]{:S(2)}, u32[]{:S(2)}) async-start(s32[8,1,2]{2,1,0:T(1,128)} %broadcast_in_dim.8), calls=%async_computation | async-start | bytes 8192 | tf_op jit(solution)/shard_map/all_to_all | solution.py:563
  6.4 0.0 copy-start
  6.4 0.0 copy-start.5
  6.4 0.0 copy-start.6
  6.4 0.1 pad_add_fusion.rank
  6.5 0.0 copy-start.2
  6.5 0.0 copy-start.3
  6.5 0.0 copy-start.4
  6.5 0.6 copy-done
  7.1 0.0 copy-done.5
  7.1 0.0 copy-done.6
  7.1 0.1 copy-done.2
  7.1 0.0 copy-done.3
  7.2 0.0 copy-done.4
  7.2 1.8 %table_a.1 = (bf16[256,256]{1,0:T(8,128)(2,1)S(1)}, bf16[256,256]{1,0:T(8,128)(2,1)S(1)}, bf16[256,256]{1,0:T(8,128)(2,1)S(1)}, bf16[256,256]{1,0:T(8,128)(2,1)S...) custom-call(s32[1,2]{1,0:T(1,128)S(1)} %copy-done.2, ...), custom_call_target="tpu_custom_call" | custom-call | flops 268435456 | bytes 1048576 | tf_op jit(solution)/shard_map/table_a/pallas_call | solution.py:541
  8.9 0.0 collective-permute-done.x
  9.0 0.7 raw.1.refs_2_
  9.7 1.9 %all-to-all-done = s32[8,1,2]{2,1,0:T(1,128)S(1)} async-done(((s32[8,1,2]{2,1,0:T(1,128)}), s32[8,1,2]{2,1,0:T(1,128)S(1)}, u32[]{:S(2)}, u32[]{:S(2)}) %all-to-all-start) | async-done | bytes 96 | tf_op jit(solution)/shard_map/all_to_all | solution.py:563
  11.5 2.7 %forward_a.1 = f32[32,8,512]{2,1,0:T(8,128)} custom-call(s32[1,2]{1,0:T(1,128)S(1)} %copy-done.2, s32[1,2]{1,0:T(1,128)S(1)} %copy-done.1, s32[2]{0:T(128)S(1)} %pad_add_fusion.rank, f32[5]{0:T(128)S(1)} %copy-done.3, f32[4]{0:T(128)S(1)} %copy-done.4, f32[5]{0:T(128)S(1)} %copy-done.5, f32[5]{0:T(128)S(1)} %copy-done.6, s32[8,2]{1,0:T(8,128)S(1)} %bitcast.13, ...), custom_call_target="tpu_custom_call" | custom-call | flops 268435456 | bytes 1048576 | tf_op jit(solution)/shard_map/forward_a/pallas_call | solution.py:541
  14.2 11.2 %all-to-all-start.1 = ((f32[32,8,512]{2,1,0:T(8,128)}), f32[32,8,512]{2,1,0:T(8,128)S(1)}, u32[]{:S(2)}, u32[]{:S(2)}) async-start(f32[32,8,512]{2,1,0:T(8,128)} %forward_a.1), calls=%async_computation.1 | async-start | bytes 1048576 | tf_op jit(solution)/shard_map/all_to_all | solution.py:567
  25.4 2.3 %table_b.1 = (bf16[256,256]{1,0:T(8,128)(2,1)S(1)}, bf16[256,256]{1,0:T(8,128)(2,1)S(1)}, bf16[256,256]{1,0:T(8,128)(2,1)S(1)}, bf16[256,256]{1,0:T(8,128)(2,1)S...) custom-call(s32[1,2]{1,0:T(1,128)S(1)} %copy-done.2, ...), custom_call_target="tpu_custom_call" | custom-call | flops 268435456 | bytes 1048576 | tf_op jit(solution)/shard_map/table_b/pallas_call | solution.py:541
  27.7 14.8 %all-to-all-done.1 = f32[32,8,512]{2,1,0:T(8,128)S(1)} async-done(((f32[32,8,512]{2,1,0:T(8,128)}), f32[32,8,512]{2,1,0:T(8,128)S(1)}, u32[]{:S(2)}, u32[]{:S(2)}) %all-to-all-start.1) | async-done | bytes 524320 | tf_op jit(solution)/shard_map/all_to_all | solution.py:567
  42.5 1.8 %both_b.1 = f32[256,512]{1,0:T(8,128)S(1)} custom-call(f32[256,512]{1,0:T(8,128)S(1)} %bitcast.11, bf16[256,256]{1,0:T(8,128)(2,1)S(1)} %get-tuple-element.39.a1h, bf16[256,256]{1,0:T(8,128)(2,1)S(1)} %get-tuple-element.40.a1l, bf16[256,256]{1,0:T(8,128)(2,1)S(1)} %get-tuple-element.41.b1h, bf16[256,256]{1,0:T(8,128)(2,1)S(1)} %get-tuple-element.42.b1l, ...), custom_call_target="tpu_custom_call" | custom-call | flops 268435456 | bytes 1048576 | tf_op jit(solution)/shard_map/both_b/pallas_call | solution.py:541
  44.4 21.4 %all_to_all.18.refs_2_ = f32[32,8,512]{2,1,0:T(8,128)S(1)} all-to-all(f32[32,8,512]{2,1,0:T(8,128)S(1)} %bitcast.12), channel_id=1, replica_groups=mesh['phase'=8,'row'=32] {'row'}, dimensions={0} | all-to-all | bytes 1048576 | tf_op jit(solution)/shard_map/all_to_all | solution.py:567
  65.8 0.0 collective-permute-start.1
  65.9 2.1 %adjoint_a.1.x = f32[2,32,1024]{2,1,0:T(8,128)S(1)} custom-call(s32[1,2]{1,0:T(1,128)S(1)} %copy-done.2, s32[1,2]{1,0:T(1,128)S(1)} %copy-done.1, s32[2]{0:T(128)S(1)} %pad_add_fusion.rank, f32[5]{0:T(128)S(1)} %copy-done.3, f32[4]{0:T(128)S(1)} %copy-done.4, f32[5]{0:T(128)S(1)} %copy-done.5, f32[5]{0:T(128)S(1)} %copy-done.6, f32[5,3,32]{2,1,0:T(4,128)S(1)} %bitcast.18, ...), custom_call_target="tpu_custom_call" | custom-call | flops 268435456 | bytes 1048576 | tf_op jit(solution)/shard_map/adjoint_a/pallas_call | solution.py:541
  67.9 4.9 %collective-permute-done.1.m = f32[32,8,256]{2,1,0:T(8,128)S(1)} collective-permute-done((f32[32,8,256]{2,1,0:T(8,128)S(1)}, f32[32,8,256]{2,1,0:T(8,128)S(1)}, u32[]{:S(2)}, u32[]{:S(2)}) %collective-permute-start.1) | collective-permute-done | bytes 262176 | tf_op jit(solution)/shard_map/ppermute | solution.py:620
  72.9 1.4 %finish.1 = f32[2,32,1024]{2,1,0:T(8,128)} custom-call(f32[2,32,1024]{2,1,0:T(8,128)S(1)} %adjoint_a.1.x, f32[32,8,256]{2,1,0:T(8,128)S(1)} %collective-permute-done.1.m), custom_call_target="tpu_custom_call" | custom-call | flops 67108864 | bytes 1048576 | tf_op jit(solution)/shard_map/finish/pallas_call | solution.py:541
  (1 shorter events, 0.0 us)
Async XLA Ops:
  0.0 2.5 %copy-start.1 = (s32[1,2]{1,0:T(1,128)S(1)}, s32[1,2]{1,0:T(1,128)}, u32[]{:S(2)}) copy-start(s32[1,2]{1,0:T(1,128)} %tick.7) | copy-start | bytes 28
  0.0 8.9 %collective-permute-start = (f32[2,32,1024]{2,1,0:T(8,128)}, f32[2,32,1024]{2,1,0:T(8,128)S(1)}, u32[]{:S(2)}, u32[]{:S(2)}) collective-permute-start(f32[2,32,1024]{2,1,0:T(8,128)} %bitcast.20), channel_id=1, source_target_pairs={{32,0},{64,32},{96,64},{128,96},{160,128},{192,160},{224,192},{0,2... | collective-permute-start | bytes 786440 | tf_op jit(solution)/shard_map/ppermute | solution.py:571
  3.1 8.5 %all-to-all-start = ((s32[8,1,2]{2,1,0:T(1,128)}), s32[8,1,2]{2,1,0:T(1,128)S(1)}, u32[]{:S(2)}, u32[]{:S(2)}) async-start(s32[8,1,2]{2,1,0:T(1,128)} %broadcast_in_dim.8), calls=%async_computation | async-start | bytes 8192 | tf_op jit(solution)/shard_map/all_to_all | solution.py:563
  6.4 0.7 copy-start
  6.4 0.7 copy-start.5
  6.4 0.7 copy-start.6
  6.5 0.7 copy-start.2
  6.5 0.7 copy-start.3
  6.5 0.7 copy-start.4
  14.2 28.4 %all-to-all-start.1 = ((f32[32,8,512]{2,1,0:T(8,128)}), f32[32,8,512]{2,1,0:T(8,128)S(1)}, u32[]{:S(2)}, u32[]{:S(2)}) async-start(f32[32,8,512]{2,1,0:T(8,128)} %forward_a.1), calls=%async_computation.1 | async-start | bytes 1048576 | tf_op jit(solution)/shard_map/all_to_all | solution.py:567
  65.8 7.0 %collective-permute-start.1 = (f32[32,8,256]{2,1,0:T(8,128)S(1)}, f32[32,8,256]{2,1,0:T(8,128)S(1)}, u32[]{:S(2)}, u32[]{:S(2)}) collective-permute-start(f32[32,8,256]{2,1,0:T(8,128)S(1)} %slice.4), channel_id=1, source_target_pairs={{0,32},{32,64},{64,96},{96,128},{128,160},{160,192},{192,224},{224... | collective-permute-start | bytes 786440 | tf_op jit(solution)/shard_map/ppermute | solution.py:620

commit v4 on v3

--- a/solution.py
+++ b/solution.py
@@ -51,12 +51,13 @@
 
 def mm(x, hi, lo, transposed=False):
     a, b = split(x)
-    return dot(a, hi, transposed) + dot(a, lo, transposed) + dot(b, hi, transposed)
+    tables = jnp.concatenate([hi, lo, hi], axis=1 if transposed else 0)
+    return dot(jnp.concatenate([a, a, b], axis=1), tables, transposed)
 
 
 def left(hi, lo, x):
     a, b = split(x)
-    return dot(hi, a) + dot(hi, b) + dot(lo, a)
+    return dot(jnp.concatenate([hi, hi, lo], axis=1), jnp.concatenate([a, b, a], axis=0))
 
 
 def pmm(x, w, transposed=False):
@@ -65,8 +66,7 @@
 
 
 def pleft(w, x):
-    a, b = split(x)
-    return dot(w, a) + dot(w, b)
+    return dot(jnp.concatenate([w, w], axis=1), jnp.concatenate(split(x), axis=0))
 
 
 def rotation(ints, pulse, step, k, width):

time: 74.7 us -> 74.6 us (level)
  no operation moved by 1% of the time
where the time goes in v4:
time: 74.6 us; the launch traced here: 74.3 us
  waiting for transfers between devices  21.6 us (29%)
  blocking collectives  21.4 us (29%)
  starting transfers between devices  17 us (23%)
  Pallas kernels  12.7 us (17%)
  local copies, waits for them, and re-layouts  1.31 us (2%)
    all_to_all x1, blocking collectives, turn(): lax.all_to_all(x.reshape(32, 8, 512), 'row', split_axis=0, concat_axis=0,...  21.4 us
    all_to_all x1, waiting for transfers between devices, turn(): lax.all_to_all(x.reshape(32, 8, 512), 'row', split_axis=0, concat_axis=0,...  14.8 us
    pallas_call x7, Pallas kernels, call(): pl.pallas_call(with_params(kernel) if scalars else kernel, in_specs=specs...  12.7 us
    all_to_all x1, starting transfers between devices, turn(): lax.all_to_all(x.reshape(32, 8, 512), 'row', split_axis=0, concat_axis=0,...  11.2 us
    ppermute x1, waiting for transfers between devices, local(): lax.ppermute(returned[:, :, 256:], 'phase', [(i, (i + 1) % phases) for i...  4.93 us
    all_to_all x1, starting transfers between devices, local(): lax.all_to_all(jnp.broadcast_to(ticks, (phases, STEPS)), 'phase', split_a...  3.31 us
    ppermute x1, starting transfers between devices, local(): lax.ppermute(current, 'phase', [((i + 1) % phases, i) for i in range(phas...  2.45 us
    all_to_all x1, waiting for transfers between devices, local(): lax.all_to_all(jnp.broadcast_to(ticks, (phases, STEPS)), 'phase', split_a...  1.86 us
  transfers between devices with their start and end apart: 4, of which 3 were waited for; matrix products, arithmetic and copies ran while one was open for 1% of the time, Pallas kernels for 9%

profile of v4, /device:TPU:32, one launch (start us, length us, event | category | flops | bytes accessed | tf_op | source)
XLA Modules:
  0.0 74.3 jit_solution(17927675702196507334)
XLA Ops:
  0.0 0.0 copy-start.1
  0.0 2.5 %collective-permute-start = (f32[2,32,1024]{2,1,0:T(8,128)}, f32[2,32,1024]{2,1,0:T(8,128)S(1)}, u32[]{:S(2)}, u32[]{:S(2)}) collective-permute-start(f32[2,32,1024]{2,1,0:T(8,128)} %bitcast.20), channel_id=1, source_target_pairs={{32,0},{64,32},{96,64},{128,96},{160,128},{192,160},{224,192},{0,2... | collective-permute-start | bytes 786440 | tf_op jit(solution)/shard_map/ppermute | solution.py:571
  2.5 0.0 copy-done.1
  2.5 0.6 broadcast_in_dim.8
  3.1 3.3 %all-to-all-start = ((s32[8,1,2]{2,1,0:T(1,128)}), s32[8,1,2]{2,1,0:T(1,128)S(1)}, u32[]{:S(2)}, u32[]{:S(2)}) async-start(s32[8,1,2]{2,1,0:T(1,128)} %broadcast_in_dim.8), calls=%async_computation | async-start | bytes 8192 | tf_op jit(solution)/shard_map/all_to_all | solution.py:563
  6.4 0.0 copy-start
  6.4 0.0 copy-start.5
  6.4 0.0 copy-start.6
  6.4 0.1 pad_add_fusion.rank
  6.5 0.0 copy-start.2
  6.5 0.0 copy-start.3
  6.5 0.0 copy-start.4
  6.5 0.6 copy-done
  7.1 0.0 copy-done.5
  7.1 0.0 copy-done.6
  7.1 0.1 copy-done.2
  7.1 0.0 copy-done.3
  7.2 0.0 copy-done.4
  7.2 1.8 %table_a.1 = (bf16[256,256]{1,0:T(8,128)(2,1)S(1)}, bf16[256,256]{1,0:T(8,128)(2,1)S(1)}, bf16[256,256]{1,0:T(8,128)(2,1)S(1)}, bf16[256,256]{1,0:T(8,128)(2,1)S...) custom-call(s32[1,2]{1,0:T(1,128)S(1)} %copy-done.2, ...), custom_call_target="tpu_custom_call" | custom-call | flops 268435456 | bytes 1048576 | tf_op jit(solution)/shard_map/table_a/pallas_call | solution.py:541
  8.9 0.0 collective-permute-done.x
  9.0 0.7 raw.1.refs_2_
  9.6 1.9 %all-to-all-done = s32[8,1,2]{2,1,0:T(1,128)S(1)} async-done(((s32[8,1,2]{2,1,0:T(1,128)}), s32[8,1,2]{2,1,0:T(1,128)S(1)}, u32[]{:S(2)}, u32[]{:S(2)}) %all-to-all-start) | async-done | bytes 96 | tf_op jit(solution)/shard_map/all_to_all | solution.py:563
  11.5 2.7 %forward_a.1 = f32[32,8,512]{2,1,0:T(8,128)} custom-call(s32[1,2]{1,0:T(1,128)S(1)} %copy-done.2, s32[1,2]{1,0:T(1,128)S(1)} %copy-done.1, s32[2]{0:T(128)S(1)} %pad_add_fusion.rank, f32[5]{0:T(128)S(1)} %copy-done.3, f32[4]{0:T(128)S(1)} %copy-done.4, f32[5]{0:T(128)S(1)} %copy-done.5, f32[5]{0:T(128)S(1)} %copy-done.6, s32[8,2]{1,0:T(8,128)S(1)} %bitcast.13, ...), custom_call_target="tpu_custom_call" | custom-call | flops 268435456 | bytes 1048576 | tf_op jit(solution)/shard_map/forward_a/pallas_call | solution.py:541
  14.2 11.2 %all-to-all-start.1 = ((f32[32,8,512]{2,1,0:T(8,128)}), f32[32,8,512]{2,1,0:T(8,128)S(1)}, u32[]{:S(2)}, u32[]{:S(2)}) async-start(f32[32,8,512]{2,1,0:T(8,128)} %forward_a.1), calls=%async_computation.1 | async-start | bytes 1048576 | tf_op jit(solution)/shard_map/all_to_all | solution.py:567
  25.4 2.3 %table_b.1 = (bf16[256,256]{1,0:T(8,128)(2,1)S(1)}, bf16[256,256]{1,0:T(8,128)(2,1)S(1)}, bf16[256,256]{1,0:T(8,128)(2,1)S(1)}, bf16[256,256]{1,0:T(8,128)(2,1)S...) custom-call(s32[1,2]{1,0:T(1,128)S(1)} %copy-done.2, ...), custom_call_target="tpu_custom_call" | custom-call | flops 268435456 | bytes 1048576 | tf_op jit(solution)/shard_map/table_b/pallas_call | solution.py:541
  27.7 14.8 %all-to-all-done.1 = f32[32,8,512]{2,1,0:T(8,128)S(1)} async-done(((f32[32,8,512]{2,1,0:T(8,128)}), f32[32,8,512]{2,1,0:T(8,128)S(1)}, u32[]{:S(2)}, u32[]{:S(2)}) %all-to-all-start.1) | async-done | bytes 524320 | tf_op jit(solution)/shard_map/all_to_all | solution.py:567
  42.5 1.8 %both_b.1 = f32[256,512]{1,0:T(8,128)S(1)} custom-call(f32[256,512]{1,0:T(8,128)S(1)} %bitcast.11, bf16[256,256]{1,0:T(8,128)(2,1)S(1)} %get-tuple-element.39.a1h, bf16[256,256]{1,0:T(8,128)(2,1)S(1)} %get-tuple-element.40.a1l, bf16[256,256]{1,0:T(8,128)(2,1)S(1)} %get-tuple-element.41.b1h, bf16[256,256]{1,0:T(8,128)(2,1)S(1)} %get-tuple-element.42.b1l, ...), custom_call_target="tpu_custom_call" | custom-call | flops 268435456 | bytes 1048576 | tf_op jit(solution)/shard_map/both_b/pallas_call | solution.py:541
  44.4 21.4 %all_to_all.18.refs_2_ = f32[32,8,512]{2,1,0:T(8,128)S(1)} all-to-all(f32[32,8,512]{2,1,0:T(8,128)S(1)} %bitcast.12), channel_id=1, replica_groups=mesh['phase'=8,'row'=32] {'row'}, dimensions={0} | all-to-all | bytes 1048576 | tf_op jit(solution)/shard_map/all_to_all | solution.py:567
  65.8 0.0 collective-permute-start.1
  65.9 2.1 %adjoint_a.1.x = f32[2,32,1024]{2,1,0:T(8,128)S(1)} custom-call(s32[1,2]{1,0:T(1,128)S(1)} %copy-done.2, s32[1,2]{1,0:T(1,128)S(1)} %copy-done.1, s32[2]{0:T(128)S(1)} %pad_add_fusion.rank, f32[5]{0:T(128)S(1)} %copy-done.3, f32[4]{0:T(128)S(1)} %copy-done.4, f32[5]{0:T(128)S(1)} %copy-done.5, f32[5]{0:T(128)S(1)} %copy-done.6, f32[5,3,32]{2,1,0:T(4,128)S(1)} %bitcast.18, ...), custom_call_target="tpu_custom_call" | custom-call | flops 268435456 | bytes 1048576 | tf_op jit(solution)/shard_map/adjoint_a/pallas_call | solution.py:541
  67.9 4.9 %collective-permute-done.1.m = f32[32,8,256]{2,1,0:T(8,128)S(1)} collective-permute-done((f32[32,8,256]{2,1,0:T(8,128)S(1)}, f32[32,8,256]{2,1,0:T(8,128)S(1)}, u32[]{:S(2)}, u32[]{:S(2)}) %collective-permute-start.1) | collective-permute-done | bytes 262176 | tf_op jit(solution)/shard_map/ppermute | solution.py:620
  72.8 1.4 %finish.1 = f32[2,32,1024]{2,1,0:T(8,128)} custom-call(f32[2,32,1024]{2,1,0:T(8,128)S(1)} %adjoint_a.1.x, f32[32,8,256]{2,1,0:T(8,128)S(1)} %collective-permute-done.1.m), custom_call_target="tpu_custom_call" | custom-call | flops 67108864 | bytes 1048576 | tf_op jit(solution)/shard_map/finish/pallas_call | solution.py:541
  (1 shorter events, 0.0 us)
Async XLA Ops:
  0.0 2.5 %copy-start.1 = (s32[1,2]{1,0:T(1,128)S(1)}, s32[1,2]{1,0:T(1,128)}, u32[]{:S(2)}) copy-start(s32[1,2]{1,0:T(1,128)} %tick.7) | copy-start | bytes 28
  0.0 8.9 %collective-permute-start = (f32[2,32,1024]{2,1,0:T(8,128)}, f32[2,32,1024]{2,1,0:T(8,128)S(1)}, u32[]{:S(2)}, u32[]{:S(2)}) collective-permute-start(f32[2,32,1024]{2,1,0:T(8,128)} %bitcast.20), channel_id=1, source_target_pairs={{32,0},{64,32},{96,64},{128,96},{160,128},{192,160},{224,192},{0,2... | collective-permute-start | bytes 786440 | tf_op jit(solution)/shard_map/ppermute | solution.py:571
  3.1 8.5 %all-to-all-start = ((s32[8,1,2]{2,1,0:T(1,128)}), s32[8,1,2]{2,1,0:T(1,128)S(1)}, u32[]{:S(2)}, u32[]{:S(2)}) async-start(s32[8,1,2]{2,1,0:T(1,128)} %broadcast_in_dim.8), calls=%async_computation | async-start | bytes 8192 | tf_op jit(solution)/shard_map/all_to_all | solution.py:563
  6.4 0.7 copy-start
  6.4 0.7 copy-start.5
  6.4 0.7 copy-start.6
  6.5 0.7 copy-start.2
  6.5 0.7 copy-start.3
  6.5 0.7 copy-start.4
  14.2 28.4 %all-to-all-start.1 = ((f32[32,8,512]{2,1,0:T(8,128)}), f32[32,8,512]{2,1,0:T(8,128)S(1)}, u32[]{:S(2)}, u32[]{:S(2)}) async-start(f32[32,8,512]{2,1,0:T(8,128)} %forward_a.1), calls=%async_computation.1 | async-start | bytes 1048576 | tf_op jit(solution)/shard_map/all_to_all | solution.py:567
  65.8 7.0 %collective-permute-start.1 = (f32[32,8,256]{2,1,0:T(8,128)S(1)}, f32[32,8,256]{2,1,0:T(8,128)S(1)}, u32[]{:S(2)}, u32[]{:S(2)}) collective-permute-start(f32[32,8,256]{2,1,0:T(8,128)S(1)} %slice.4), channel_id=1, source_target_pairs={{0,32},{32,64},{64,96},{96,128},{128,160},{160,192},{192,224},{224... | collective-permute-start | bytes 786440 | tf_op jit(solution)/shard_map/ppermute | solution.py:620

commit v5 on v4

--- a/solution.py
+++ b/solution.py
@@ -69,16 +69,32 @@
     return dot(jnp.concatenate([w, w], axis=1), jnp.concatenate(split(x), axis=0))
 
 
-def rotation(ints, pulse, step, k, width):
-    sc = [sincos(jnp.full((1, width), pulse[k, m, ints[step]], F32)) for m in range(3)]
-    (s0, c0), (s1, c1), (s2, c2) = sc
+def rotations(ints, pulse, which, width):
+    count = -(-3 * len(which) // 8) * 8
+    row = iota((count, 128), 0)
+    theta = jnp.zeros((count, 128), F32)
+    for n, (step, k) in enumerate(which):
+        for m in range(3):
+            theta = jnp.where(row == 3 * n + m, pulse[k, m, ints[step]], theta)
+    sines, cosines = sincos(theta)
     zero = jnp.zeros((1, width), F32)
-    return [
-        [c0, -s0 * c1, s0 * s1 * c2, -s0 * s1 * s2],
-        [s0, c0 * c1, -c0 * s1 * c2, c0 * s1 * s2],
-        [zero, s1, c1 * c2, -c1 * s2],
-        [zero, zero, s2, c2],
-    ]
+
+    def splat(table, n):
+        return jnp.concatenate([table[n : n + 1, :]] * (width // 128), axis=1)
+
+    out = []
+    for n in range(len(which)):
+        s0, s1, s2 = (splat(sines, 3 * n + m) for m in range(3))
+        c0, c1, c2 = (splat(cosines, 3 * n + m) for m in range(3))
+        out.append(
+            [
+                [c0, -s0 * c1, s0 * s1 * c2, -s0 * s1 * s2],
+                [s0, c0 * c1, -c0 * s1 * c2, c0 * s1 * s2],
+                [zero, s1, c1 * c2, -c1 * s2],
+                [zero, zero, s2, c2],
+            ]
+        )
+    return out
 
 
 def identity(width):
@@ -181,8 +197,9 @@
     natural = [(lane >> 6) & 3, (lane >> 4) & 3, (lane >> 2) & 3, lane & 3]
     moved = moved_lanes(lane)
     eye = identity(w)
-    first = [rotation(ints, pulse, 0, k, w) for k in range(TRANSMONS)]
-    second = {k: rotation(ints, pulse, 1, k, w) for k in (3, 4)}
+    which = [(0, k) for k in range(TRANSMONS)] + [(1, 3), (1, 4)]
+    *first, third, fourth = rotations(ints, pulse, which, w)
+    second = {3: third, 4: fourth}
     store_kron(w1h, w1l, [flip(first[k]) for k in (1, 2, 3, 4)], natural)
     store_kron(w2h, w2l, [eye, eye, flip(second[3]), flip(second[4])], moved)
     store_rows_a(k1h, k1l, first[0], first[3], first[4])
@@ -420,7 +437,7 @@
         lane & 3,
         (lane >> 3) & 3,
     ]
-    first = [flip(rotation(ints, pulse, 0, k, 256)) for k in (0, 3, 4)]
+    first = [flip(o) for o in rotations(ints, pulse, [(0, k) for k in (0, 3, 4)], 256)]
     store_kron(t1h, t1l, [first[0], identity(256), first[1], first[2]], sent)
     both = to_lanes(left(t1h[...], t1l[...], rows))
     fr, fi = first_factor(ints, fl, start_of(ints, gathered) + F32(0.5) * fnum(ints[2]))
@@ -443,8 +460,9 @@
     lane = iota((1, w), 1)
     natural = [(lane >> 6) & 3, (lane >> 4) & 3, (lane >> 2) & 3, lane & 3]
     eye = identity(w)
-    first = [rotation(ints, pulse, 0, k, w) for k in range(3)]
-    second = [rotation(ints, pulse, 1, k, w) for k in range(4)]
+    which = [(0, k) for k in range(3)] + [(1, k) for k in range(4)]
+    both = rotations(ints, pulse, which, w)
+    first, second = both[:3], both[3:]
     store_kron(a1h, a1l, [*first, eye], natural)
     store_kron(b1h, b1l, [*(flip(o) for o in first), eye], natural)
     store_kron(a2h, a2l, second, natural)

time: 74.6 us -> 74.6 us (level)
  no operation moved by 1% of the time
where the time goes in v5:
time: 74.6 us; the launch traced here: 74.3 us
  waiting for transfers between devices  21.7 us (29%)
  blocking collectives  21.4 us (29%)
  starting transfers between devices  17 us (23%)
  Pallas kernels  12.7 us (17%)
  local copies, waits for them, and re-layouts  1.31 us (2%)
    all_to_all x1, blocking collectives, turn(): lax.all_to_all(x.reshape(32, 8, 512), 'row', split_axis=0, concat_axis=0,...  21.4 us
    all_to_all x1, waiting for transfers between devices, turn(): lax.all_to_all(x.reshape(32, 8, 512), 'row', split_axis=0, concat_axis=0,...  14.9 us
    pallas_call x7, Pallas kernels, call(): pl.pallas_call(with_params(kernel) if scalars else kernel, in_specs=specs...  12.7 us
    all_to_all x1, starting transfers between devices, turn(): lax.all_to_all(x.reshape(32, 8, 512), 'row', split_axis=0, concat_axis=0,...  11.2 us
    ppermute x1, waiting for transfers between devices, local(): lax.ppermute(returned[:, :, 256:], 'phase', [(i, (i + 1) % phases) for i...  4.94 us
    all_to_all x1, starting transfers between devices, local(): lax.all_to_all(jnp.broadcast_to(ticks, (phases, STEPS)), 'phase', split_a...  3.31 us
    ppermute x1, starting transfers between devices, local(): lax.ppermute(current, 'phase', [((i + 1) % phases, i) for i in range(phas...  2.45 us
    all_to_all x1, waiting for transfers between devices, local(): lax.all_to_all(jnp.broadcast_to(ticks, (phases, STEPS)), 'phase', split_a...  1.86 us
  transfers between devices with their start and end apart: 4, of which 3 were waited for; matrix products, arithmetic and copies ran while one was open for 1% of the time, Pallas kernels for 9%

profile of v5, /device:TPU:32, one launch (start us, length us, event | category | flops | bytes accessed | tf_op | source)
XLA Modules:
  0.0 74.3 jit_solution(17765353996371262764)
XLA Ops:
  0.0 0.0 copy-start.1
  0.0 2.5 %collective-permute-start = (f32[2,32,1024]{2,1,0:T(8,128)}, f32[2,32,1024]{2,1,0:T(8,128)S(1)}, u32[]{:S(2)}, u32[]{:S(2)}) collective-permute-start(f32[2,32,1024]{2,1,0:T(8,128)} %bitcast.20), channel_id=1, source_target_pairs={{32,0},{64,32},{96,64},{128,96},{160,128},{192,160},{224,192},{0,2... | collective-permute-start | bytes 786440 | tf_op jit(solution)/shard_map/ppermute | solution.py:589
  2.5 0.0 copy-done.1
  2.5 0.6 broadcast_in_dim.8
  3.1 3.3 %all-to-all-start = ((s32[8,1,2]{2,1,0:T(1,128)}), s32[8,1,2]{2,1,0:T(1,128)S(1)}, u32[]{:S(2)}, u32[]{:S(2)}) async-start(s32[8,1,2]{2,1,0:T(1,128)} %broadcast_in_dim.8), calls=%async_computation | async-start | bytes 8192 | tf_op jit(solution)/shard_map/all_to_all | solution.py:581
  6.4 0.0 copy-start
  6.4 0.0 copy-start.5
  6.4 0.0 copy-start.6
  6.4 0.1 pad_add_fusion.rank
  6.5 0.0 copy-start.2
  6.5 0.0 copy-start.3
  6.5 0.0 copy-start.4
  6.5 0.6 copy-done
  7.1 0.0 copy-done.5
  7.1 0.0 copy-done.6
  7.1 0.1 copy-done.2
  7.1 0.0 copy-done.3
  7.2 0.0 copy-done.4
  7.2 1.8 %table_a.1 = (bf16[256,256]{1,0:T(8,128)(2,1)S(1)}, bf16[256,256]{1,0:T(8,128)(2,1)S(1)}, bf16[256,256]{1,0:T(8,128)(2,1)S(1)}, bf16[256,256]{1,0:T(8,128)(2,1)S...) custom-call(s32[1,2]{1,0:T(1,128)S(1)} %copy-done.2, ...), custom_call_target="tpu_custom_call" | custom-call | flops 268435456 | bytes 1048576 | tf_op jit(solution)/shard_map/table_a/pallas_call | solution.py:559
  8.9 0.0 collective-permute-done.x
  9.0 0.7 raw.1.refs_2_
  9.6 1.9 %all-to-all-done = s32[8,1,2]{2,1,0:T(1,128)S(1)} async-done(((s32[8,1,2]{2,1,0:T(1,128)}), s32[8,1,2]{2,1,0:T(1,128)S(1)}, u32[]{:S(2)}, u32[]{:S(2)}) %all-to-all-start) | async-done | bytes 96 | tf_op jit(solution)/shard_map/all_to_all | solution.py:581
  11.5 2.7 %forward_a.1 = f32[32,8,512]{2,1,0:T(8,128)} custom-call(s32[1,2]{1,0:T(1,128)S(1)} %copy-done.2, s32[1,2]{1,0:T(1,128)S(1)} %copy-done.1, s32[2]{0:T(128)S(1)} %pad_add_fusion.rank, f32[5]{0:T(128)S(1)} %copy-done.3, f32[4]{0:T(128)S(1)} %copy-done.4, f32[5]{0:T(128)S(1)} %copy-done.5, f32[5]{0:T(128)S(1)} %copy-done.6, s32[8,2]{1,0:T(8,128)S(1)} %bitcast.13, ...), custom_call_target="tpu_custom_call" | custom-call | flops 268435456 | bytes 1048576 | tf_op jit(solution)/shard_map/forward_a/pallas_call | solution.py:559
  14.2 11.2 %all-to-all-start.1 = ((f32[32,8,512]{2,1,0:T(8,128)}), f32[32,8,512]{2,1,0:T(8,128)S(1)}, u32[]{:S(2)}, u32[]{:S(2)}) async-start(f32[32,8,512]{2,1,0:T(8,128)} %forward_a.1), calls=%async_computation.1 | async-start | bytes 1048576 | tf_op jit(solution)/shard_map/all_to_all | solution.py:585
  25.4 2.3 %table_b.1 = (bf16[256,256]{1,0:T(8,128)(2,1)S(1)}, bf16[256,256]{1,0:T(8,128)(2,1)S(1)}, bf16[256,256]{1,0:T(8,128)(2,1)S(1)}, bf16[256,256]{1,0:T(8,128)(2,1)S...) custom-call(s32[1,2]{1,0:T(1,128)S(1)} %copy-done.2, ...), custom_call_target="tpu_custom_call" | custom-call | flops 268435456 | bytes 1048576 | tf_op jit(solution)/shard_map/table_b/pallas_call | solution.py:559
  27.6 14.9 %all-to-all-done.1 = f32[32,8,512]{2,1,0:T(8,128)S(1)} async-done(((f32[32,8,512]{2,1,0:T(8,128)}), f32[32,8,512]{2,1,0:T(8,128)S(1)}, u32[]{:S(2)}, u32[]{:S(2)}) %all-to-all-start.1) | async-done | bytes 524320 | tf_op jit(solution)/shard_map/all_to_all | solution.py:585
  42.5 1.8 %both_b.1 = f32[256,512]{1,0:T(8,128)S(1)} custom-call(f32[256,512]{1,0:T(8,128)S(1)} %bitcast.11, bf16[256,256]{1,0:T(8,128)(2,1)S(1)} %get-tuple-element.39.a1h, bf16[256,256]{1,0:T(8,128)(2,1)S(1)} %get-tuple-element.40.a1l, bf16[256,256]{1,0:T(8,128)(2,1)S(1)} %get-tuple-element.41.b1h, bf16[256,256]{1,0:T(8,128)(2,1)S(1)} %get-tuple-element.42.b1l, ...), custom_call_target="tpu_custom_call" | custom-call | flops 268435456 | bytes 1048576 | tf_op jit(solution)/shard_map/both_b/pallas_call | solution.py:559
  44.4 21.4 %all_to_all.18.refs_2_ = f32[32,8,512]{2,1,0:T(8,128)S(1)} all-to-all(f32[32,8,512]{2,1,0:T(8,128)S(1)} %bitcast.12), channel_id=1, replica_groups=mesh['phase'=8,'row'=32] {'row'}, dimensions={0} | all-to-all | bytes 1048576 | tf_op jit(solution)/shard_map/all_to_all | solution.py:585
  65.8 0.0 collective-permute-start.1
  65.9 2.0 %adjoint_a.1.x = f32[2,32,1024]{2,1,0:T(8,128)S(1)} custom-call(s32[1,2]{1,0:T(1,128)S(1)} %copy-done.2, s32[1,2]{1,0:T(1,128)S(1)} %copy-done.1, s32[2]{0:T(128)S(1)} %pad_add_fusion.rank, f32[5]{0:T(128)S(1)} %copy-done.3, f32[4]{0:T(128)S(1)} %copy-done.4, f32[5]{0:T(128)S(1)} %copy-done.5, f32[5]{0:T(128)S(1)} %copy-done.6, f32[5,3,32]{2,1,0:T(4,128)S(1)} %bitcast.18, ...), custom_call_target="tpu_custom_call" | custom-call | flops 268435456 | bytes 1048576 | tf_op jit(solution)/shard_map/adjoint_a/pallas_call | solution.py:559
  67.9 4.9 %collective-permute-done.1.m = f32[32,8,256]{2,1,0:T(8,128)S(1)} collective-permute-done((f32[32,8,256]{2,1,0:T(8,128)S(1)}, f32[32,8,256]{2,1,0:T(8,128)S(1)}, u32[]{:S(2)}, u32[]{:S(2)}) %collective-permute-start.1) | collective-permute-done | bytes 262176 | tf_op jit(solution)/shard_map/ppermute | solution.py:638
  72.8 1.4 %finish.1 = f32[2,32,1024]{2,1,0:T(8,128)} custom-call(f32[2,32,1024]{2,1,0:T(8,128)S(1)} %adjoint_a.1.x, f32[32,8,256]{2,1,0:T(8,128)S(1)} %collective-permute-done.1.m), custom_call_target="tpu_custom_call" | custom-call | flops 67108864 | bytes 1048576 | tf_op jit(solution)/shard_map/finish/pallas_call | solution.py:559
  (1 shorter events, 0.0 us)
Async XLA Ops:
  0.0 2.5 %copy-start.1 = (s32[1,2]{1,0:T(1,128)S(1)}, s32[1,2]{1,0:T(1,128)}, u32[]{:S(2)}) copy-start(s32[1,2]{1,0:T(1,128)} %tick.7) | copy-start | bytes 28
  0.0 8.9 %collective-permute-start = (f32[2,32,1024]{2,1,0:T(8,128)}, f32[2,32,1024]{2,1,0:T(8,128)S(1)}, u32[]{:S(2)}, u32[]{:S(2)}) collective-permute-start(f32[2,32,1024]{2,1,0:T(8,128)} %bitcast.20), channel_id=1, source_target_pairs={{32,0},{64,32},{96,64},{128,96},{160,128},{192,160},{224,192},{0,2... | collective-permute-start | bytes 786440 | tf_op jit(solution)/shard_map/ppermute | solution.py:589
  3.1 8.5 %all-to-all-start = ((s32[8,1,2]{2,1,0:T(1,128)}), s32[8,1,2]{2,1,0:T(1,128)S(1)}, u32[]{:S(2)}, u32[]{:S(2)}) async-start(s32[8,1,2]{2,1,0:T(1,128)} %broadcast_in_dim.8), calls=%async_computation | async-start | bytes 8192 | tf_op jit(solution)/shard_map/all_to_all | solution.py:581
  6.4 0.7 copy-start
  6.4 0.7 copy-start.5
  6.4 0.7 copy-start.6
  6.5 0.7 copy-start.2
  6.5 0.7 copy-start.3
  6.5 0.7 copy-start.4
  14.2 28.4 %all-to-all-start.1 = ((f32[32,8,512]{2,1,0:T(8,128)}), f32[32,8,512]{2,1,0:T(8,128)S(1)}, u32[]{:S(2)}, u32[]{:S(2)}) async-start(f32[32,8,512]{2,1,0:T(8,128)} %forward_a.1), calls=%async_computation.1 | async-start | bytes 1048576 | tf_op jit(solution)/shard_map/all_to_all | solution.py:585
  65.8 7.0 %collective-permute-start.1 = (f32[32,8,256]{2,1,0:T(8,128)S(1)}, f32[32,8,256]{2,1,0:T(8,128)S(1)}, u32[]{:S(2)}, u32[]{:S(2)}) collective-permute-start(f32[32,8,256]{2,1,0:T(8,128)S(1)} %slice.4), channel_id=1, source_target_pairs={{0,32},{32,64},{64,96},{96,128},{128,160},{160,192},{192,224},{224... | collective-permute-start | bytes 786440 | tf_op jit(solution)/shard_map/ppermute | solution.py:638
